TPU v7x, 128 devices: a whole 4x4x4 slice. The times are simulated.
128 devices in a mesh: seq: 16 (over y, z), grp: 8 (over x, core).
Axes of the slice: x: 4, y: 4, z: 4, core: 2. Of those that a mesh axis runs over, the one named last changes fastest.
Arguments:
- queries: bfloat16 [16384, 1024], P(('grp', 'seq')), may hold values from -160 to 160
- states: bfloat16 [16384, 1024], P(('grp', 'seq')), may hold values from -6 to 6
- behavior_keys: bfloat16 [16, 4096, 1024], P('grp', 'seq'), may hold values from -7 to 7
- behavior_values: bfloat16 [16, 4096, 1024], P('grp', 'seq'), may hold values from -6 to 6
- lengths: int32 [16], P('grp'), may hold values from 1024 to 4096, as said below
- user_of: int32 [16384], P('grp'), may hold values from 0 to 1
- out_weight: bfloat16 [1024, 1024], replicated, may hold values from -0.1875 to 0.1875
- norm_gain: float32 [1024], replicated, may hold values from 0.1 to 1.9
- routes: int32 [16384, 2], P(('grp', 'seq')), may hold values from 0 to 127, all different within a row; in each aligned block of 256 rows (0 to 255, 256 to 511, ...) at most 4 rows name the same one
- route_weights: float32 [16384, 2], P(('grp', 'seq')), may hold values from 0.25 to 1
- expert_up: bfloat16 [128, 1024, 4096], P(('seq', 'grp')), may hold values from -0.1875 to 0.1875
- expert_down: bfloat16 [128, 4096, 1024], P(('seq', 'grp')), may hold values from -0.09375 to 0.09375
Outputs:
- block_out: bfloat16 [16384, 1024], P(('grp', 'seq'))
Inputs may be any that keep to these rules, and one draw needn't show every extreme that they name: For the tokens of one device, no expert is named by more than 4 of their routes. `lengths`: some user has all 4096 behaviors valid in every draw.
All inputs are finite; a program needn't handle non-finite values.
Results may differ from a plain program's by a relative error of at most 0.0065.
Values may be sent and summed in bfloat16 or wider, within the bound.
A program may use at most 128 MiB of HBM per device.

v0:
```python
import math

import jax
import jax.numpy as jnp
from jax import lax
from jax.sharding import PartitionSpec as P

HEADS = 8


def copy_for_each(value, axis):
    copies = jnp.broadcast_to(value, (lax.axis_size(axis), *value.shape))
    return lax.all_to_all(copies, axis, split_axis=0, concat_axis=0, tiled=True)


def taken_together(value, axis):
    everything = copy_for_each(value, axis)
    return jnp.max(everything, axis=0)


def side_by_side(arrays, axis, split_dim, concat_dim, along):
    widths = [a.shape[along] for a in arrays]
    both = jnp.concatenate(arrays, axis=along)
    result = lax.all_to_all(both, axis, split_axis=split_dim, concat_axis=concat_dim, tiled=True)
    return tuple(jnp.split(result, [sum(widths[:k]) for k in range(1, len(widths))], axis=along))


def in_blocks(value, dim, size):
    shape = value.shape
    parts = value.reshape(*shape[:dim], size, shape[dim] // size, *shape[dim + 1 :])
    return jnp.moveaxis(parts, dim, 0)


def in_order(parts, dim):
    parts = jnp.moveaxis(parts, 0, dim)
    shape = parts.shape
    return parts.reshape(*shape[:dim], shape[dim] * shape[dim + 1], *shape[dim + 2 :])


def one_exchange(value, axis, axes, splits, concats):
    sizes = [lax.axis_size(a) for a in axes]
    parts = in_blocks(value, splits[0], sizes[0])
    parts = jnp.moveaxis(in_blocks(parts, splits[1] + 1, sizes[1]), 0, 1)
    inside = parts.shape[2:]
    parts = parts.reshape(-1, *inside)
    parts = lax.all_to_all(parts, axis, split_axis=0, concat_axis=0, tiled=True)
    parts = in_order(parts.reshape(*sizes, *inside), concats[0] + 1)
    return in_order(parts, concats[1])


def head_layout(rows, ratio):
    users, hist_local, width = rows.shape
    sub = hist_local // ratio
    shaped = rows.reshape(users, ratio, sub, HEADS, width // HEADS)
    return jnp.transpose(shaped, (3, 1, 0, 2, 4)).reshape(HEADS * ratio, users, sub, width // HEADS)


def attend_heads(queries, behavior_keys, behavior_values, lengths, user_of):
    seq_count = lax.axis_size("seq")
    ratio = seq_count // HEADS
    tok_count, width = queries.shape
    head_size = width // HEADS
    hist_local = behavior_keys.shape[1]
    sub = hist_local // ratio
    head = lax.axis_index("seq") // ratio
    portion = lax.axis_index("seq") % ratio
    keys_head, values_head = (
        lax.all_to_all(
            head_layout(behavior_keys, ratio), "seq", split_axis=0, concat_axis=2, tiled=True
        ),
        lax.all_to_all(
            head_layout(behavior_values, ratio), "seq", split_axis=0, concat_axis=2, tiled=True
        ),
    )
    keys_head = keys_head[0]
    values_head = values_head[0]
    spread_heads = jnp.repeat(queries.reshape(tok_count, HEADS, head_size), ratio, axis=1)
    query_send = jnp.transpose(spread_heads, (1, 0, 2))
    query_head = lax.all_to_all(query_send, "seq", split_axis=0, concat_axis=0, tiled=True).reshape(
        -1, head_size
    )
    positions = (
        jnp.arange(seq_count, dtype=jnp.int32)[:, None] * hist_local
        + portion * sub
        + jnp.arange(sub, dtype=jnp.int32)[None, :]
    ).reshape(-1)
    factor = 1.0 / math.sqrt(head_size)
    listing = []
    for member in range(keys_head.shape[0]):
        scores = (
            jnp.einsum(
                "gd,pd->gp", query_head, keys_head[member], preferred_element_type=jnp.float32
            )
            * factor
        )
        usable = (user_of == member)[:, None] & (positions < lengths[member])[None, :]
        listing.append((jnp.where(usable, scores, -1e30), usable))
    local_peak = listing[0][0].max(-1)
    for scores, usable in listing[1:]:
        local_peak = jnp.maximum(local_peak, scores.max(-1))
    columns = jnp.arange(HEADS, dtype=jnp.int32)[None, :]
    placed = jnp.where(columns == head, local_peak[:, None], -1e30)
    every_peak = taken_together(placed.astype(jnp.bfloat16), "seq").astype(placed.dtype)
    peaks = lax.dynamic_slice_in_dim(every_peak, head, 1, 1)[:, 0]
    numer = None
    denom = None
    for member in range(len(listing)):
        scores, usable = listing[member]
        probs = jnp.where(usable, jnp.exp(scores - peaks[:, None]), 0.0)
        term = jnp.dot(
            probs.astype(jnp.bfloat16), values_head[member], preferred_element_type=jnp.float32
        )
        if numer is None:
            numer, denom = (term, probs.sum(-1))
        else:
            numer, denom = (numer + term, denom + probs.sum(-1))
    numer_back, denom_back = tuple(
        (
            part.astype(jnp.float32)
            for part in side_by_side(
                (
                    numer.reshape(seq_count, tok_count, head_size).astype(jnp.bfloat16),
                    denom.reshape(seq_count, tok_count, 1).astype(jnp.bfloat16),
                ),
                "seq",
                0,
                0,
                2,
            )
        )
    )
    numer_own = numer_back.reshape(HEADS, ratio, tok_count, head_size).sum(1)
    denom_own = denom_back.reshape(HEADS, ratio, tok_count).sum(1)
    return (jnp.transpose(numer_own, (1, 0, 2)), jnp.transpose(denom_own, (1, 0)))


def body(
    queries,
    states,
    behavior_keys,
    behavior_values,
    lengths,
    user_of,
    out_weight,
    norm_gain,
    routes,
    route_weights,
    expert_up,
    expert_down,
):
    tok_count = queries.shape[0]
    numer, denom = attend_heads(queries, behavior_keys, behavior_values, lengths, user_of)
    attended = (numer / denom[..., None]).reshape(queries.shape).astype(jnp.bfloat16)
    residual = states.astype(jnp.float32) + jnp.dot(
        attended, out_weight, preferred_element_type=jnp.float32
    )
    spread = jnp.mean(residual * residual, axis=-1, keepdims=True)
    normed = (residual / jnp.sqrt(spread + 1e-06) * norm_gain).astype(jnp.bfloat16)
    seq_count = lax.axis_size("seq")
    grp_count = lax.axis_size("grp")
    experts_all = seq_count * grp_count
    width = normed.shape[1]
    top = routes.shape[1]
    capacity = max(2, 2 * tok_count * top // experts_all)
    flat = routes.reshape(-1)
    onehot = (flat[:, None] == jnp.arange(experts_all, dtype=jnp.int32)[None, :]).astype(jnp.int32)
    earlier = jnp.cumsum(onehot, axis=0) - onehot
    slots = jnp.sum(earlier * onehot, axis=1)
    target = flat * capacity + slots
    rows = jnp.broadcast_to(normed[:, None, :], (tok_count, top, width)).reshape(-1, width)
    buffer = jnp.zeros((experts_all * capacity, width), jnp.bfloat16).at[target].set(rows)
    stacked = buffer.reshape(seq_count, grp_count, capacity, width)
    received = one_exchange(stacked, ("seq", "grp"), ("seq", "grp"), (0, 1), (0, 1))
    shape = received.shape
    flat_rows = received.reshape(-1, shape[-1])
    hidden = jax.nn.gelu(
        jnp.dot(flat_rows, expert_up[0], preferred_element_type=jnp.float32)
    ).astype(jnp.bfloat16)
    answered = one_exchange(
        jnp.dot(hidden, expert_down[0], preferred_element_type=jnp.float32)
        .astype(jnp.bfloat16)
        .reshape(shape),
        ("seq", "grp"),
        ("seq", "grp"),
        (0, 1),
        (0, 1),
    )
    picked = answered.reshape(-1, width)[target].astype(jnp.float32).reshape(tok_count, top, width)
    mixed = jnp.sum(picked * route_weights[:, :, None], axis=1)
    return (residual + mixed).astype(jnp.bfloat16)


def solution(mesh):
    return jax.shard_map(
        body,
        mesh=mesh,
        in_specs=(
            P(("grp", "seq"), None),
            P(("grp", "seq"), None),
            P("grp", "seq", None),
            P("grp", "seq", None),
            P("grp"),
            P("grp"),
            P(),
            P(),
            P(("grp", "seq"), None),
            P(("grp", "seq"), None),
            P(("seq", "grp"), None, None),
            P(("seq", "grp"), None, None),
        ),
        out_specs=P(("grp", "seq"), None),
        check_vma=False,
    )
```

profile of v0, /device:TPU:1, one launch (start us, length us, event | category | flops | bytes accessed | tf_op | source)
XLA Modules:
  0.0 214.3 jit_solution(5449617624897321890)
XLA Ops:
  0.0 1.6 copy.50
  2.9 8.6 %all-to-all-start.1 = ((bf16[16,2,128,128]{3,2,1,0:T(8,128)(2,1)}), bf16[16,2,128,128]{3,2,1,0:T(8,128)(2,1)S(1)}, u32[]{:S(2)}, u32[]{:S(2)}) async-start(bf16[16,2,128,128]{3,2,1,0:T(8,128)(2,1)} %bitcast.116), calls=%async_computation.1 | async-start | bytes 2097152 | tf_op jit(solution)/shard_map/all_to_all | solution.py:68
  17.1 10.1 %all-to-all-done.1 = bf16[16,2,128,128]{3,2,1,0:T(8,128)(2,1)S(1)} async-done(((bf16[16,2,128,128]{3,2,1,0:T(8,128)(2,1)}), bf16[16,2,128,128]{3,2,1,0:T(8,128)(2,1)S(1)}, u32[]{:S(2)}, u32[]{:S(2)}) %all-to-all-start.1) | async-done | bytes 1048608 | tf_op jit(solution)/shard_map/all_to_all | solution.py:68
  28.0 4.3 %all-to-all-start = ((bf16[16,128,128]{2,1,0:T(8,128)(2,1)}), bf16[16,128,128]{2,1,0:T(8,128)(2,1)}, u32[]{:S(2)}, u32[]{:S(2)}) async-start(bf16[16,128,128]{2,1,0:T(8,128)(2,1)} %bitcast.124), calls=%async_computation | async-start | bytes 1048576 | tf_op jit(solution)/shard_map/all_to_all | solution.py:79
  33.0 1.5 copy.51
  36.9 4.4 %all-to-all-done = bf16[16,128,128]{2,1,0:T(8,128)(2,1)} async-done(((bf16[16,128,128]{2,1,0:T(8,128)(2,1)}), bf16[16,128,128]{2,1,0:T(8,128)(2,1)}, u32[]{:S(2)}, u32[]{:S(2)}) %all-to-all-start) | async-done | bytes 524320 | tf_op jit(solution)/shard_map/all_to_all | solution.py:79
  41.3 3.7 %all-to-all-start.3 = ((bf16[16,2,128,128]{3,2,1,0:T(8,128)(2,1)}), bf16[16,2,128,128]{3,2,1,0:T(8,128)(2,1)S(1)}, u32[]{:S(2)}, u32[]{:S(2)}) async-start(bf16[16,2,128,128]{3,2,1,0:T(8,128)(2,1)} %bitcast.118), calls=%async_computation.3 | async-start | bytes 2097152 | tf_op jit(solution)/shard_map/all_to_all | solution.py:71
  44.9 8.5 %fusion = (bf16[2048]{0:T(1024)(128)(2,1)S(1)}, f32[2048,2048]{0,1:T(8,128)}) fusion(pred[2048]{0:T(1024)(128)(4,1)S(1)} %get-tuple-element.12, pred[2048]{0:T(1024)(128)(4,1)S(1)} %get-tuple-element.14, bf16[2048,128]{1,0:T(8,128)(2,1)} %bitcast.4, bf16[2048,128]{1,0:T(8,128)(2,1)} %bitcast.133), kind=kOutput, calls=%fused_computation.6 | convolution fusion | flops 1090516992 | bytes 17833984 | tf_op jit(solution)/shard_map/gd,pd->gp/dot_general | solution.py:91
  53.5 8.4 %fusion.1 = (bf16[2048]{0:T(1024)(128)(2,1)S(1)}, f32[2048,2048]{0,1:T(8,128)}) fusion(pred[2048]{0:T(1024)(128)(4,1)S(1)} %get-tuple-element.11, pred[2048]{0:T(1024)(128)(4,1)S(1)} %get-tuple-element.13, bf16[2048,128]{1,0:T(8,128)(2,1)} %bitcast.4, bf16[2048,128]{1,0:T(8,128)(2,1)S(1)} %bitcast.132), kind=kOutput, calls=%fused_computation.7 | convolution fusion | flops 1090516992 | bytes 17833984 | tf_op jit(solution)/shard_map/gd,pd->gp/dot_general | solution.py:91
  62.9 6.7 %all-to-all-start.2 = ((bf16[16,2048,8]{1,2,0:T(8,128)(2,1)}), bf16[16,2048,8]{1,2,0:T(8,128)(2,1)}, u32[]{:S(2)}, u32[]{:S(2)}) async-start(bf16[16,2048,8]{1,2,0:T(8,128)(2,1)} %broadcast_in_dim.64), calls=%async_computation.2 | async-start | bytes 1048576 | tf_op jit(solution)/shard_map/all_to_all | solution.py:13
  70.6 7.9 %all-to-all-done.2 = bf16[16,2048,8]{1,2,0:T(8,128)(2,1)} async-done(((bf16[16,2048,8]{1,2,0:T(8,128)(2,1)}), bf16[16,2048,8]{1,2,0:T(8,128)(2,1)}, u32[]{:S(2)}, u32[]{:S(2)}) %all-to-all-start.2) | async-done | bytes 524320 | tf_op jit(solution)/shard_map/all_to_all | solution.py:13
  79.7 9.0 %fusion.18 = f32[2048,128]{1,0:T(8,128)S(1)} fusion(bf16[2048,128]{1,0:T(8,128)(2,1)} %bitcast.134, f32[2048,2048]{0,1:T(8,128)} %get-tuple-element.20, f32[2048]{0:T(1024)S(1)} %bitcast.135, pred[2048]{0:T(1024)(128)(4,1)S(1)} %get-tuple-element.11, pred[2048]{0:T(1024)(128)(4,1)S(1)} %get-tuple-element.13), kind=kOutput, calls=%fused_computation.25 | convolution fusion | flops 1098907648 | bytes 18362368 | tf_op jit(solution)/shard_map/dot_general | solution.py:110
  88.8 15.6 %fusion.4 = (f32[2048]{0:T(1024)S(1)}, f32[2048]{0:T(1024)S(1)}) fusion(f32[2048,2048]{0,1:T(8,128)} %get-tuple-element.20, f32[2048]{0:T(1024)S(1)} %bitcast.136, pred[2048]{0:T(1024)(128)(4,1)S(1)} %get-tuple-element.11, pred[2048]{0:T(1024)(128)(4,1)S(1)} %get-tuple-element.13, f32[2048,2048]{0,1:T(8,128)} %get-tuple-element.18, ...), kind=kLoop, calls=%fused_computation.11 | loop fusion | flops 50327552 | bytes 33587200 | tf_op jit(solution)/shard_map/reduce_sum | solution.py:116
  104.4 6.3 %fusion.33 = bf16[2048,128]{1,0:T(8,128)(2,1)S(1)} fusion(f32[2048,128]{1,0:T(8,128)S(1)} %fusion.18, bf16[2048,128]{1,0:T(8,128)(2,1)S(1)} %bitcast.131, f32[2048,2048]{0,1:T(8,128)S(1)} %bitcast.114, f32[2048]{0:T(1024)S(1)} %bitcast.137, pred[2048]{0:T(1024)(128)(4,1)} %copy-done.9, pred[2048]{0:T(1024)(128)(4,1)} %copy-done.8), kind=kOutput, calls=%fused_computation.35 | convolution fusion | flops 1099431936 | bytes 18886656 | tf_op jit(solution)/shard_map/dot_general | solution.py:110
  111.9 3.8 %all-to-all-start.4 = ((bf16[16,128,129]{1,2,0:T(8,128)(2,1)}), bf16[16,128,129]{1,2,0:T(8,128)(2,1)S(1)}, u32[]{:S(2)}, u32[]{:S(2)}) async-start(bf16[16,128,129]{1,2,0:T(8,128)(2,1)} %pad_maximum_fusion), calls=%async_computation.4 | async-start | bytes 1114112 | tf_op jit(solution)/shard_map/all_to_all | solution.py:24
  117.5 7.1 %all-to-all-done.4 = bf16[16,128,129]{1,2,0:T(8,128)(2,1)S(1)} async-done(((bf16[16,128,129]{1,2,0:T(8,128)(2,1)}), bf16[16,128,129]{1,2,0:T(8,128)(2,1)S(1)}, u32[]{:S(2)}, u32[]{:S(2)}) %all-to-all-start.4) | async-done | bytes 528416 | tf_op jit(solution)/shard_map/all_to_all | solution.py:24
  128.5 2.4 %scatter_custom_fusion = bf16[512,1024]{1,0:T(8,128)(2,1)S(1)} fusion(s32[256]{0:T(256)S(1)} %bitcast.142, bf16[256,1024]{1,0:T(8,128)(2,1)} %reshape.229, bf16[]{:T(256)} %constant.64.clone.1), kind=kCustom, calls=%fused_computation.47 | custom fusion | bytes 1049088 | tf_op jit(solution)/shard_map/scatter | solution.py:171
  132.1 31.7 %all_to_all.55 = bf16[128,1,1,4,1024]{4,3,2,1,0:T(4,128)(2,1)S(1)} all-to-all(bf16[128,1,1,4,1024]{4,3,2,1,0:T(4,128)(2,1)} %reshape_transpose_transpose_reshape_reshape_reshape.6), channel_id=1, replica_groups=mesh['seq'=16,'grp'=8] {'seq','grp'}, dimensions={0} | all-to-all | bytes 2097152 | tf_op jit(solution)/shard_map/all_to_all | solution.py:46
  164.9 15.0 %fusion.40 = bf16[512,1024]{1,0:T(8,128)(2,1)S(1)} fusion(bf16[1,4096,1024]{2,1,0:T(8,128)(2,1)} %param.23, bf16[512,1024]{1,0:T(8,128)(2,1)} %reshape_reshape.6, bf16[1,1024,4096]{2,1,0:T(8,128)(2,1)} %param.22), kind=kOutput, calls=%fused_computation.36 | convolution fusion | flops 8609333248 | bytes 18874368 | tf_op jit(solution)/shard_map/dot_general | solution.py:180
  181.2 4.6 %all-to-all-start.6 = ((bf16[128,1,1,4,1024]{4,3,2,1,0:T(4,128)(2,1)}), bf16[128,1,1,4,1024]{4,3,2,1,0:T(4,128)(2,1)S(1)}, u32[]{:S(2)}, u32[]{:S(2)}) async-start(bf16[128,1,1,4,1024]{4,3,2,1,0:T(4,128)(2,1)} %bitcast.120), calls=%async_computation.6 | async-start | bytes 2097152 | tf_op jit(solution)/shard_map/all_to_all | solution.py:46
  185.9 19.2 %all-to-all-done.6 = bf16[128,1,1,4,1024]{4,3,2,1,0:T(4,128)(2,1)S(1)} async-done(((bf16[128,1,1,4,1024]{4,3,2,1,0:T(4,128)(2,1)}), bf16[128,1,1,4,1024]{4,3,2,1,0:T(4,128)(2,1)S(1)}, u32[]{:S(2)}, u32[]{:S(2)}) %all-to-all-start.6) | async-done | bytes 1048608 | tf_op jit(solution)/shard_map/all_to_all | solution.py:46
  207.5 2.0 gather_fusion
  209.4 1.7 reshape.216
  212.5 1.8 add_convert_fusion
  (91 shorter events, 28.1 us)
Async XLA Ops:
  0.0 125.0 %copy-start = (bf16[1024,1024]{1,0:T(8,128)(2,1)S(1)}, bf16[1024,1024]{1,0:T(8,128)(2,1)}, u32[]{:S(2)}) copy-start(bf16[1024,1024]{1,0:T(8,128)(2,1)} %param.18) | copy-start | bytes 6291460
  0.0 35.8 %copy-start.10 = (s32[2048]{0:T(1024)S(1)}, s32[2048]{0:T(1024)}, u32[]{:S(2)}) copy-start(s32[2048]{0:T(1024)} %param.17) | copy-start | bytes 24580
  2.9 24.3 %all-to-all-start.1 = ((bf16[16,2,128,128]{3,2,1,0:T(8,128)(2,1)}), bf16[16,2,128,128]{3,2,1,0:T(8,128)(2,1)S(1)}, u32[]{:S(2)}, u32[]{:S(2)}) async-start(bf16[16,2,128,128]{3,2,1,0:T(8,128)(2,1)} %bitcast.116), calls=%async_computation.1 | async-start | bytes 2097152 | tf_op jit(solution)/shard_map/all_to_all | solution.py:68
  14.1 0.7 copy-start.3
  16.1 72.6 %copy-start.8 = (pred[2048]{0:T(1024)(128)(4,1)}, pred[2048]{0:T(1024)(128)(4,1)S(1)}, u32[]{:S(2)}) copy-start(pred[2048]{0:T(1024)(128)(4,1)S(1)} %get-tuple-element.14) | copy-start | bytes 6148
  28.0 13.2 %all-to-all-start = ((bf16[16,128,128]{2,1,0:T(8,128)(2,1)}), bf16[16,128,128]{2,1,0:T(8,128)(2,1)}, u32[]{:S(2)}, u32[]{:S(2)}) async-start(bf16[16,128,128]{2,1,0:T(8,128)(2,1)} %bitcast.124), calls=%async_computation | async-start | bytes 1048576 | tf_op jit(solution)/shard_map/all_to_all | solution.py:79
  35.8 17.6 %copy-start.11 = (s32[128,3]{0,1:T(4,128)}, s32[128,3]{0,1:T(4,128)S(1)}, u32[]{:S(2)}) copy-start(s32[128,3]{0,1:T(4,128)S(1)} %reduce-window.9) | copy-start | bytes 4612
  35.8 52.9 %copy-start.9 = (pred[2048]{0:T(1024)(128)(4,1)}, pred[2048]{0:T(1024)(128)(4,1)S(1)}, u32[]{:S(2)}) copy-start(pred[2048]{0:T(1024)(128)(4,1)S(1)} %get-tuple-element.12) | copy-start | bytes 6148
  41.3 20.7 %all-to-all-start.3 = ((bf16[16,2,128,128]{3,2,1,0:T(8,128)(2,1)}), bf16[16,2,128,128]{3,2,1,0:T(8,128)(2,1)S(1)}, u32[]{:S(2)}, u32[]{:S(2)}) async-start(bf16[16,2,128,128]{3,2,1,0:T(8,128)(2,1)} %bitcast.118), calls=%async_computation.3 | async-start | bytes 2097152 | tf_op jit(solution)/shard_map/all_to_all | solution.py:71
  44.9 8.5 %copy-start.6 = (bf16[1,1,16,128,128]{4,3,1,2,0:T(8,128)(2,1)S(1)}, bf16[1,1,16,128,128]{4,3,1,2,0:T(8,128)(2,1)}, u32[]{:S(2)}) copy-start(bf16[1,1,16,128,128]{4,3,1,2,0:T(8,128)(2,1)} %get-tuple-element.10) | copy-start | bytes 1572868
  53.4 16.1 %slice-start.4 = ((s32[128,3]{0,1:T(4,128)}), s32[128,2]{0,1:T(2,128)S(1)}, s32[]{:S(2)}) async-start(s32[128,3]{0,1:T(4,128)} %copy-done.11), calls=%async_computation.11 | async-start | bytes 2048 | tf_op jit(solution)/shard_map/slice.1
  53.5 16.1 %copy-start.4 = (s32[128,2,128]{0,1,2:T(2,128)S(1)}, s32[128,2,128]{0,1,2:T(2,128)}, u32[]{:S(2)}) copy-start(s32[128,2,128]{0,1,2:T(2,128)} %copy-done.3) | copy-start | bytes 393220
  62.9 15.7 %all-to-all-start.2 = ((bf16[16,2048,8]{1,2,0:T(8,128)(2,1)}), bf16[16,2048,8]{1,2,0:T(8,128)(2,1)}, u32[]{:S(2)}, u32[]{:S(2)}) async-start(bf16[16,2048,8]{1,2,0:T(8,128)(2,1)} %broadcast_in_dim.64), calls=%async_computation.2 | async-start | bytes 1048576 | tf_op jit(solution)/shard_map/all_to_all | solution.py:13
  79.7 24.7 %slice-start = ((s8[16777216]{0:T(1024)(128)(4,1)}), s8[4194304]{0:T(1024)(128)(4,1)S(1)}, s32[]{:S(2)}) async-start(s8[16777216]{0:T(1024)(128)(4,1)} %bitcast.113), calls=%async_computation.7 | async-start | bytes 8388608
  79.7 24.7 %slice-start.1 = ((s8[16777216]{0:T(1024)(128)(4,1)}), s8[4194304]{0:T(1024)(128)(4,1)S(1)}, s32[]{:S(2)}) async-start(s8[16777216]{0:T(1024)(128)(4,1)} %bitcast.113), calls=%async_computation.8 | async-start | bytes 8388608
  79.7 24.7 %slice-start.2 = ((s8[16777216]{0:T(1024)(128)(4,1)}), s8[4194304]{0:T(1024)(128)(4,1)S(1)}, s32[]{:S(2)}) async-start(s8[16777216]{0:T(1024)(128)(4,1)} %bitcast.113), calls=%async_computation.9 | async-start | bytes 8388608
  88.8 15.6 %slice-start.3 = ((s8[16777216]{0:T(1024)(128)(4,1)}), s8[4194304]{0:T(1024)(128)(4,1)S(1)}, s32[]{:S(2)}) async-start(s8[16777216]{0:T(1024)(128)(4,1)} %bitcast.113), calls=%async_computation.10 | async-start | bytes 8388608
  88.8 15.6 %copy-start.5 = (bf16[1,1,16,128,128]{4,3,1,2,0:T(8,128)(2,1)S(1)}, bf16[1,1,16,128,128]{4,3,1,2,0:T(8,128)(2,1)}, u32[]{:S(2)}) copy-start(bf16[1,1,16,128,128]{4,3,1,2,0:T(8,128)(2,1)} %get-tuple-element.7) | copy-start | bytes 1572868
  104.4 20.6 %copy-start.7 = (bf16[128,1024]{1,0:T(8,128)(2,1)S(1)}, bf16[128,1024]{1,0:T(8,128)(2,1)}, u32[]{:S(2)}) copy-start(bf16[128,1024]{1,0:T(8,128)(2,1)} %param.13) | copy-start | bytes 786436
  111.9 12.7 %all-to-all-start.4 = ((bf16[16,128,129]{1,2,0:T(8,128)(2,1)}), bf16[16,128,129]{1,2,0:T(8,128)(2,1)S(1)}, u32[]{:S(2)}, u32[]{:S(2)}) async-start(bf16[16,128,129]{1,2,0:T(8,128)(2,1)} %pad_maximum_fusion), calls=%async_computation.4 | async-start | bytes 1114112 | tf_op jit(solution)/shard_map/all_to_all | solution.py:24
  125.6 0.8 copy-start.1
  164.9 20.9 %copy-start.12 = (f32[128,2]{0,1:T(2,128)S(1)}, f32[128,2]{0,1:T(2,128)}, u32[]{:S(2)}) copy-start(f32[128,2]{0,1:T(2,128)} %param.21) | copy-start | bytes 3076
  181.2 24.0 %all-to-all-start.6 = ((bf16[128,1,1,4,1024]{4,3,2,1,0:T(4,128)(2,1)}), bf16[128,1,1,4,1024]{4,3,2,1,0:T(4,128)(2,1)S(1)}, u32[]{:S(2)}, u32[]{:S(2)}) async-start(bf16[128,1,1,4,1024]{4,3,2,1,0:T(4,128)(2,1)} %bitcast.120), calls=%async_computation.6 | async-start | bytes 2097152 | tf_op jit(solution)/shard_map/all_to_all | solution.py:46
  205.2 1.0 copy-start.2
where the time goes:
time: 215 us; the launch traced here: 214 us
  waiting for transfers between devices  48.6 us (23%)
  matrix products  47.8 us (22%)
  blocking collectives  31.7 us (15%)
  starting transfers between devices  31.6 us (15%)
  local copies, waits for them, and re-layouts  28.9 us (13%)
  other arithmetic  25.2 us (12%)
    all_to_all x1, blocking collectives, one_exchange(): parts = lax.all_to_all(parts, axis, split_axis=0, concat_axis=0, tiled=True)  31.7 us
    all_to_all x1, waiting for transfers between devices, one_exchange(): parts = lax.all_to_all(parts, axis, split_axis=0, concat_axis=0, tiled=True)  19.2 us
    dot_general x2, matrix products, attend_heads(): jnp.einsum('gd,pd->gp', query_head, keys_head[member], preferred_element_...  16.9 us
    reduce_sum x1, other arithmetic, attend_heads(): numer, denom = (numer + term, denom + probs.sum(-1))  15.6 us
    dot_general x2, matrix products, attend_heads(): jnp.dot(probs.astype(jnp.bfloat16), values_head[member], preferred_elemen...  15.3 us
    dot_general x1, matrix products, body(): jnp.dot(hidden, expert_down[0], preferred_element_type=jnp.float32)  15 us
    all_to_all x1, waiting for transfers between devices, attend_heads(): lax.all_to_all(head_layout(behavior_keys, ratio), 'seq', split_axis=0, co...  10.1 us
    all_to_all x1, starting transfers between devices, attend_heads(): lax.all_to_all(head_layout(behavior_keys, ratio), 'seq', split_axis=0, co...  8.59 us
  transfers between devices with their start and end apart: 6, of which 5 were waited for; matrix products, arithmetic and copies ran while one was open for 14% of the time, Pallas kernels for 0%

commit v1 on v0

v1 whole, which is shorter than its diff:
```python
import functools
import math

import jax
import jax.numpy as jnp
from jax import lax
from jax.experimental import pallas as pl
from jax.experimental.pallas import tpu as pltpu
from jax.sharding import PartitionSpec as P

HEADS = 8
MESH = pl.DeviceIdType.MESH
BF = jnp.bfloat16
F32 = jnp.float32
LOW = -1e30

FULL = ((0, 1), (0, 3), (1, 0), (3, 0))
FIRST = ((1, 1), (1, 3), (2, 0))
SECOND = ((3, 3), (3, 1), (0, 2))
HALVES = FIRST + SECOND


def head_of(y, z):
    return (y % 2) * 4 + (z + 2 * (y // 2)) % 4


def seq_of(y, z):
    return ((y + 8) % 4) * 4 + (z + 8) % 4


def cols(head, width=128):
    return pl.ds(pl.multiple_of(head * width, width), width)


def attention_kernel(
    q_hbm, k_hbm, v_hbm, len_ref, user_ref, routes_ref,
    att_ref, partner_ref,
    q_v, k_v, v_v, qbuf, kcat, vcat, qt, score, prob, osend, obuf, ssend, sbuf, rbuf,
    load_sem, own_sem, qs, qr, ks, kr, vs, vr, os, orr, ss, sr, rs, rr,
):
    me = lax.axis_index("seq")
    y, z = me // 4, me % 4
    head = head_of(y, z)
    hist = k_hbm.shape[1]
    half = hist // 2
    tok = q_hbm.shape[0]
    count = 16
    width = 128
    scale = math.log2(math.e) / math.sqrt(width)

    loads = [
        pltpu.make_async_copy(src, dst, load_sem.at[i])
        for i, (src, dst) in enumerate(((q_hbm, q_v), (k_hbm, k_v), (v_hbm, v_v)))
    ]
    for copy in loads:
        copy.start()
    own = [pltpu.make_async_copy(q_hbm.at[:, cols(head)], qbuf.at[me], own_sem.at[0])]
    for i, (src, dst) in enumerate(((k_hbm, kcat), (v_hbm, vcat))):
        for user in range(2):
            own.append(
                pltpu.make_async_copy(
                    src.at[user, :, cols(head)],
                    dst.at[pl.ds(0, hist), pl.ds(user * width, width)],
                    own_sem.at[1 + 2 * i + user],
                )
            )
    for copy in own:
        copy.start()

    barrier = pltpu.get_barrier_semaphore()
    for step in range(1, count):
        pl.semaphore_signal(
            barrier, inc=1, device_id={"seq": (me + step) % count}, device_id_type=MESH
        )
    pl.semaphore_wait(barrier, count - 1)

    partner = me + 1 - 2 * (me % 2)
    route_copy = pltpu.make_async_remote_copy(
        src_ref=routes_ref, dst_ref=rbuf, send_sem=rs, recv_sem=rr,
        device_id={"seq": partner}, device_id_type=MESH,
    )
    route_copy.start()

    loads[0].wait()
    for dy in range(4):
        for dz in range(4):
            if dy == 0 and dz == 0:
                continue
            ty, tz = (y + dy) % 4, (z + dz) % 4
            pltpu.make_async_remote_copy(
                src_ref=q_v.at[:, cols(head_of(ty, tz))],
                dst_ref=qbuf.at[me],
                send_sem=qs, recv_sem=qr,
                device_id={"seq": ty * 4 + tz}, device_id_type=MESH,
            ).start()

    def send_rows(src, dst, send_sem, recv_sem):
        for j, (dy, dz) in enumerate(HALVES):
            ty, tz = (y - dy + 4) % 4, (z - dz + 4) % 4
            first = 0 if (dy, dz) in FIRST else half
            for user in range(2):
                pltpu.make_async_remote_copy(
                    src_ref=src.at[user, pl.ds(first, half), cols(head_of(ty, tz))],
                    dst_ref=dst.at[pl.ds(5 * hist + j * half, half), pl.ds(user * width, width)],
                    send_sem=send_sem, recv_sem=recv_sem,
                    device_id={"seq": ty * 4 + tz}, device_id_type=MESH,
                ).start()
        for j, (dy, dz) in enumerate(FULL):
            ty, tz = (y - dy + 4) % 4, (z - dz + 4) % 4
            for user in range(2):
                pltpu.make_async_remote_copy(
                    src_ref=src.at[user, :, cols(head_of(ty, tz))],
                    dst_ref=dst.at[pl.ds((1 + j) * hist, hist), pl.ds(user * width, width)],
                    send_sem=send_sem, recv_sem=recv_sem,
                    device_id={"seq": ty * 4 + tz}, device_id_type=MESH,
                ).start()

    loads[1].wait()
    send_rows(k_v, kcat, ks, kr)
    loads[2].wait()
    send_rows(v_v, vcat, vs, vr)

    starts = []
    for dy, dz in ((0, 0),) + FULL:
        base = seq_of(y + dy, z + dz) * hist
        starts += [base, base + half]
    for dy, dz in HALVES:
        base = seq_of(y + dy, z + dz) * hist
        starts.append(base if (dy, dz) in FIRST else base + half)

    own[0].wait()
    moved = pl.ds(0, count - 1)
    pltpu.make_async_copy(qbuf.at[moved], qbuf.at[moved], qr).wait()
    for i in range(count):
        flipped = qbuf[i].T
        users = user_ref[:, i * tok : (i + 1) * tok]
        for user in range(2):
            qt[user * width : (user + 1) * width, i * tok : (i + 1) * tok] = jnp.where(
                users == user, flipped, jnp.zeros_like(flipped)
            )

    rest = pl.ds(hist, kcat.shape[0] - hist)
    own[1].wait()
    own[2].wait()
    pltpu.make_async_copy(kcat.at[rest], kcat.at[rest], kr).wait()

    tokens = count * tok
    block = 4 * tok
    limit0 = len_ref[0, 0]
    limit1 = len_ref[0, 1]
    stat = {}
    for b in range(tokens // block):
        here = pl.ds(b * block, block)
        users = user_ref[:, b * block : (b + 1) * block]
        limit = jnp.where(users == 0, limit0, limit1)
        top = jnp.full((8, block), LOW, F32)
        for c, start in enumerate(starts):
            s = jnp.dot(kcat[c * half : (c + 1) * half, :], qt[:, here], preferred_element_type=F32)
            pos = start + lax.broadcasted_iota(jnp.int32, (half, block), 0)
            s = jnp.where(pos < limit, s, LOW)
            score[c * half : (c + 1) * half, :] = s
            top = jnp.maximum(top, s.reshape(half // 8, 8, block).max(0))
        peak = top.max(0, keepdims=True)
        total = jnp.zeros((8, block), F32)
        for c in range(len(starts)):
            p = jnp.exp2((score[c * half : (c + 1) * half, :] - peak) * scale)
            total = total + p.reshape(half // 8, 8, block).sum(0)
            prob[c * half : (c + 1) * half, here] = p.astype(BF)
        stat[b] = (peak, total.sum(0, keepdims=True))

    own[3].wait()
    own[4].wait()
    pltpu.make_async_copy(vcat.at[rest], vcat.at[rest], vr).wait()

    for b in range(tokens // block):
        here = pl.ds(b * block, block)
        users = user_ref[:, b * block : (b + 1) * block]
        both = lax.dot_general(
            vcat[...], prob[:, here], (((0,), (0,)), ((), ())), preferred_element_type=F32
        )
        peak, total = stat[b]
        out = jnp.where(users == 0, both[:width], both[width:]) * (1.0 / total)
        out = out.astype(BF)
        packed = jnp.concatenate([peak, total, jnp.zeros((6, block), F32)], axis=0)
        for i in range(block // tok):
            owner = b * (block // tok) + i
            osend[owner] = out[:, i * tok : (i + 1) * tok]
            ssend[owner] = packed[:, i * tok : (i + 1) * tok]
        for i in range(block // tok):
            owner = b * (block // tok) + i

            @pl.when(owner != me)
            def _(owner=owner):
                pltpu.make_async_remote_copy(
                    src_ref=osend.at[owner], dst_ref=obuf.at[me], send_sem=os, recv_sem=orr,
                    device_id={"seq": owner}, device_id_type=MESH,
                ).start()
                pltpu.make_async_remote_copy(
                    src_ref=ssend.at[owner], dst_ref=sbuf.at[me], send_sem=ss, recv_sem=sr,
                    device_id={"seq": owner}, device_id_type=MESH,
                ).start()

    obuf[me] = osend[me]
    sbuf[me] = ssend[me]
    route_copy.wait()
    partner_ref[...] = rbuf[...]
    pltpu.make_async_copy(qbuf.at[moved], qbuf.at[moved], qs).wait()
    pltpu.make_async_copy(kcat.at[rest], kcat.at[rest], ks).wait()
    pltpu.make_async_copy(vcat.at[rest], vcat.at[rest], vs).wait()
    pltpu.make_async_copy(obuf.at[moved], obuf.at[moved], os).wait()
    pltpu.make_async_copy(sbuf.at[moved], sbuf.at[moved], ss).wait()
    pltpu.make_async_copy(obuf.at[moved], obuf.at[moved], orr).wait()
    pltpu.make_async_copy(sbuf.at[moved], sbuf.at[moved], sr).wait()

    for h in range(HEADS):
        hy, hz = h // 4, h % 4
        first = hy * 4 + hz
        second = (hy + 2) * 4 + (hz + 2) % 4
        m0, d0 = sbuf[first, 0:1], sbuf[first, 1:2]
        m1, d1 = sbuf[second, 0:1], sbuf[second, 1:2]
        top = jnp.maximum(m0, m1)
        w0 = d0 * jnp.exp2((m0 - top) * scale)
        w1 = d1 * jnp.exp2((m1 - top) * scale)
        inverse = 1.0 / (w0 + w1)
        merged = obuf[first].astype(F32) * (w0 * inverse) + obuf[second].astype(F32) * (w1 * inverse)
        att_ref[h * width : (h + 1) * width, :] = merged.astype(BF)


def attention(queries, keys, values, lengths, users, routes):
    tok, model = queries.shape
    hist = keys.shape[1]
    width = model // HEADS
    rows = 8 * hist
    count = 16
    any_spec = pl.BlockSpec(memory_space=pl.ANY)
    vmem = pl.BlockSpec(memory_space=pltpu.VMEM)
    smem = pl.BlockSpec(memory_space=pltpu.SMEM)
    dma = pltpu.SemaphoreType.DMA
    return pl.pallas_call(
        attention_kernel,
        out_shape=(
            jax.ShapeDtypeStruct((model, tok), BF),
            jax.ShapeDtypeStruct((2, tok), jnp.int32),
        ),
        in_specs=[any_spec, any_spec, any_spec, smem, vmem, vmem],
        out_specs=(vmem, vmem),
        scratch_shapes=[
            pltpu.VMEM((tok, model), BF),
            pltpu.VMEM((2, hist, model), BF),
            pltpu.VMEM((2, hist, model), BF),
            pltpu.VMEM((count, tok, width), BF),
            pltpu.VMEM((rows, 2 * width), BF),
            pltpu.VMEM((rows, 2 * width), BF),
            pltpu.VMEM((2 * width, count * tok), BF),
            pltpu.VMEM((rows, 4 * tok), F32),
            pltpu.VMEM((rows, count * tok), BF),
            pltpu.VMEM((count, width, tok), BF),
            pltpu.VMEM((count, width, tok), BF),
            pltpu.VMEM((count, 8, tok), F32),
            pltpu.VMEM((count, 8, tok), F32),
            pltpu.VMEM((2, tok), jnp.int32),
            dma((3,)),
            dma((5,)),
        ]
        + [dma] * 12,
        compiler_params=pltpu.CompilerParams(
            collective_id=0, has_side_effects=True, vmem_limit_bytes=48 * 1024 * 1024
        ),
        name="attention",
    )(queries, keys, values, lengths, users, routes)


def experts_kernel(
    att_ref, partner_ref, routes_ref, gates_ref, states_ref, gain_ref, wo_hbm, up_hbm, down_hbm,
    out_ref,
    wo, up, down, send, recv, hidden, back, answer,
    load_sem, ds, dr, bs, br,
):
    s, g = lax.axis_index("seq"), lax.axis_index("grp")
    seqs, grps = 16, 8
    total = seqs * grps
    me = s * grps + g
    parity = s % 2
    pair = g * (seqs // 2) + s // 2
    tok, model = states_ref.shape
    ff = up.shape[1]
    loads = [
        pltpu.make_async_copy(src, dst, load_sem.at[i])
        for i, (src, dst) in enumerate(((wo_hbm, wo), (up_hbm.at[0], up), (down_hbm.at[0], down)))
    ]
    for copy in loads:
        copy.start()

    barrier = pltpu.get_barrier_semaphore()

    def greet(i, carry):
        other = (me + i) % total
        pl.semaphore_signal(
            barrier, inc=1, device_id={"seq": other // grps, "grp": other % grps},
            device_id_type=MESH,
        )
        return carry

    lax.fori_loop(1, total, greet, 0)

    experts = lax.broadcasted_iota(jnp.int32, (total, tok), 0)
    named = [(routes_ref[k : k + 1, :] == experts).astype(F32) for k in range(2)]
    others = sum((partner_ref[k : k + 1, :] == experts).astype(F32) for k in range(2))
    earlier = (
        lax.broadcasted_iota(jnp.int32, (tok, tok), 0) < lax.broadcasted_iota(jnp.int32, (tok, tok), 1)
    ).astype(BF)
    rank = jnp.dot((named[0] + named[1]).astype(BF), earlier, preferred_element_type=F32)
    ahead = jnp.dot(others.astype(BF), jnp.ones((tok, tok), BF), preferred_element_type=F32)
    rank = rank + ahead * parity.astype(F32)
    places = lax.broadcasted_iota(jnp.int32, (4 * total, tok), 0)
    onehot = []
    for k in range(2):
        slot = jnp.sum(named[k] * rank, axis=0, keepdims=True).astype(jnp.int32)
        target = routes_ref[k : k + 1, :] * 4 + slot
        onehot.append((places == target).astype(F32).astype(BF))
    placed = onehot[0] + onehot[1]

    loads[0].wait()
    residual = states_ref[...].astype(F32) + lax.dot_general(
        att_ref[...], wo[...], (((0,), (0,)), ((), ())), preferred_element_type=F32
    )
    spread = jnp.mean(residual * residual, axis=-1, keepdims=True)
    normed = (residual / jnp.sqrt(spread + 1e-06) * gain_ref[...]).astype(BF)
    send[...] = (
        jnp.dot(placed, normed, preferred_element_type=F32).reshape(total, 4, model).astype(BF)
    )

    pl.semaphore_wait(barrier, total - 1)

    def dispatch(i, carry):
        other = (me + i) % total
        pltpu.make_async_remote_copy(
            src_ref=send.at[other], dst_ref=recv.at[parity, pair], send_sem=ds, recv_sem=dr,
            device_id={"seq": other // grps, "grp": other % grps}, device_id_type=MESH,
        ).start()
        return carry

    lax.fori_loop(1, total, dispatch, 0)
    recv[parity, pair] = send[me]
    loads[1].wait()
    loads[2].wait()
    moved = pl.ds(0, total - 1)
    pltpu.make_async_copy(answer.at[moved], answer.at[moved], dr).wait()
    rows = (recv[0].astype(F32) + recv[1].astype(F32)).reshape(2 * total, model).astype(BF)
    step = 512
    for j in range(ff // step):
        hidden[:, j * step : (j + 1) * step] = jax.nn.gelu(
            jnp.dot(rows, up[:, j * step : (j + 1) * step], preferred_element_type=F32)
        ).astype(BF)
    step = 256
    for j in range(model // step):
        back[:, :, j * step : (j + 1) * step] = (
            jnp.dot(hidden[...], down[:, j * step : (j + 1) * step], preferred_element_type=F32)
            .reshape(total // 2, 4, step)
            .astype(BF)
        )

    def reply(i, carry):
        other = (me + i) % total
        os, og = other // grps, other % grps
        pltpu.make_async_remote_copy(
            src_ref=back.at[og * (seqs // 2) + os // 2], dst_ref=answer.at[me],
            send_sem=bs, recv_sem=br,
            device_id={"seq": os, "grp": og}, device_id_type=MESH,
        ).start()
        return carry

    lax.fori_loop(1, total, reply, 0)
    answer[me] = back[pair]
    pltpu.make_async_copy(answer.at[moved], answer.at[moved], ds).wait()
    pltpu.make_async_copy(answer.at[moved], answer.at[moved], bs).wait()
    pltpu.make_async_copy(answer.at[moved], answer.at[moved], br).wait()
    answers = answer[...].astype(F32).reshape(4 * total, model).astype(BF)
    mixed = residual
    for k in range(2):
        picked = lax.dot_general(
            onehot[k], answers, (((0,), (0,)), ((), ())), preferred_element_type=F32
        )
        mixed = mixed + picked * gates_ref[:, k : k + 1]
    out_ref[...] = mixed.astype(BF)


def experts(att, partner, routes, gates, states, gain, out_weight, up, down):
    tok, model = states.shape
    ff = up.shape[2]
    total = 128
    any_spec = pl.BlockSpec(memory_space=pl.ANY)
    vmem = pl.BlockSpec(memory_space=pltpu.VMEM)
    dma = pltpu.SemaphoreType.DMA
    return pl.pallas_call(
        experts_kernel,
        out_shape=jax.ShapeDtypeStruct((tok, model), BF),
        in_specs=[vmem] * 6 + [any_spec] * 3,
        out_specs=vmem,
        scratch_shapes=[
            pltpu.VMEM((model, model), BF),
            pltpu.VMEM((model, ff), BF),
            pltpu.VMEM((ff, model), BF),
            pltpu.VMEM((total, 4, model), BF),
            pltpu.VMEM((2, total // 2, 4, model), BF),
            pltpu.VMEM((2 * total, ff), BF),
            pltpu.VMEM((total // 2, 4, model), BF),
            pltpu.VMEM((total, 4, model), BF),
            dma((3,)),
        ]
        + [dma] * 4,
        compiler_params=pltpu.CompilerParams(
            collective_id=1, has_side_effects=True, vmem_limit_bytes=56 * 1024 * 1024
        ),
        name="experts",
    )(att, partner, routes, gates, states, gain, out_weight, up, down)


def body(
    queries, states, behavior_keys, behavior_values, lengths, user_of, out_weight, norm_gain,
    routes, route_weights, expert_up, expert_down,
):
    routes_t = routes.T
    att, partner = attention(
        queries, behavior_keys, behavior_values, lengths.reshape(1, -1), user_of.reshape(1, -1),
        routes_t,
    )
    return experts(
        att, partner, routes_t, route_weights, states, norm_gain.reshape(1, -1), out_weight,
        expert_up, expert_down,
    )


def solution(mesh):
    return jax.shard_map(
        body,
        mesh=mesh,
        in_specs=(
            P(("grp", "seq"), None),
            P(("grp", "seq"), None),
            P("grp", "seq", None),
            P("grp", "seq", None),
            P("grp"),
            P("grp"),
            P(),
            P(),
            P(("grp", "seq"), None),
            P(("grp", "seq"), None),
            P(("seq", "grp"), None, None),
            P(("seq", "grp"), None, None),
        ),
        out_specs=P(("grp", "seq"), None),
        check_vma=False,
    )
```

time: 215 us -> 98.7 us (0.46)
  Pallas kernels: 0 us -> 88.6 us
  waiting for transfers between devices: 48.6 us -> 0 us
  matrix products: 47.8 us -> 0 us
  blocking collectives: 31.7 us -> 0 us
  starting transfers between devices: 31.6 us -> 0 us
  other arithmetic: 25.2 us -> 0 us
  local copies, waits for them, and re-layouts: 28.9 us -> 9.79 us
    pallas_call x0 -> x2, Pallas kernels: none -> 88.6 us  [the longest x1 50.5 us: experts(): pl.pallas_call(experts_kernel, out_shape=jax.ShapeDtypeStruct((tok, model...]
    all_to_all x6 -> x0, waiting for transfers between devices: 48.6 us -> none  [the longest x1 19.2 us: one_exchange(): parts = lax.all_to_all(parts, axis, split_axis=0, concat_axis=0, tiled=True)]
    dot_general x6 -> x0, matrix products: 47.8 us -> none  [the longest x2 16.9 us: attend_heads(): jnp.einsum('gd,pd->gp', query_head, keys_head[member], preferred_element_...]
    all_to_all x1 -> x0, blocking collectives: 31.7 us -> none  [one_exchange(): parts = lax.all_to_all(parts, axis, split_axis=0, concat_axis=0, tiled=True)]
    all_to_all x6 -> x0, starting transfers between devices: 31.6 us -> none  [the longest x1 8.59 us: attend_heads(): lax.all_to_all(head_layout(behavior_keys, ratio), 'seq', split_axis=0, co...]
    reduce_sum x5 -> x0, other arithmetic: 17.9 us -> none  [the longest x1 15.6 us: attend_heads(): numer, denom = (numer + term, denom + probs.sum(-1))]
    another operation x8 -> x0, local copies, waits for them, and re-layouts: 4.88 us -> none  [the longest x2 2.43 us: one_exchange(): parts = parts.reshape(-1, *inside)]
    slice x3 -> x0, local copies, waits for them, and re-layouts: 3.44 us -> none  [the longest x1 1.34 us: attend_heads(): lengths[member]]
  transfers between devices with their start and end apart: 6 -> 0, of which waited for: 5 -> 0; matrix products, arithmetic and copies ran while one was open for 14% -> 0% of each run, Pallas kernels for 0% -> 0%
where the time goes in v1:
time: 98.7 us; the launch traced here: 98.4 us
  Pallas kernels  88.6 us (90%)
  local copies, waits for them, and re-layouts  9.79 us (10%)
    pallas_call x1, Pallas kernels, experts(): pl.pallas_call(experts_kernel, out_shape=jax.ShapeDtypeStruct((tok, model...  50.5 us
    pallas_call x1, Pallas kernels, attention(): pl.pallas_call(attention_kernel, out_shape=(jax.ShapeDtypeStruct((model,...  38.1 us
    unnamed x18, local copies, waits for them, and re-layouts  9.79 us

profile of v1, /device:TPU:1, one launch (start us, length us, event | category | flops | bytes accessed | tf_op | source)
XLA Modules:
  0.0 98.4 jit_solution(1962842336888413961)
XLA Ops:
  0.0 1.4 %copy.13.gates_ref = f32[128,2]{1,0:T(8,128)} copy(f32[128,2]{0,1:T(2,128)} %param.21) | data formatting | bytes 2048 | tf_op args[9]
  1.4 0.0 copy-start
  1.4 1.2 %copy-done = bf16[2,256,1024]{2,1,0:T(8,128)(2,1)S(1)} copy-done((bf16[2,256,1024]{2,1,0:T(8,128)(2,1)S(1)}, bf16[2,256,1024]{2,1,0:T(8,128)(2,1)}, u32[]{:S(2)}) %copy-start) | copy-done | bytes 1048600
  2.6 0.0 copy-start.1
  2.6 1.2 %copy-done.1 = bf16[2,256,1024]{2,1,0:T(8,128)(2,1)S(1)} copy-done((bf16[2,256,1024]{2,1,0:T(8,128)(2,1)S(1)}, bf16[2,256,1024]{2,1,0:T(8,128)(2,1)}, u32[]{:S(2)}) %copy-start.1) | copy-done | bytes 1048600
  3.9 0.0 copy-start.3
  3.9 0.9 copy-done.3
  4.8 0.0 copy-start.4
  4.8 0.7 copy-done.4
  5.5 0.0 copy-start.5
  5.5 0.7 copy-done.5
  6.2 0.0 copy-start.7
  6.2 0.7 copy-done.7
  6.8 38.1 %attention.1 = (bf16[1024,128]{1,0:T(8,128)(2,1)S(1)}, s32[2,128]{1,0:T(2,128)S(1)}) custom-call(bf16[128,1024]{1,0:T(8,128)(2,1)S(1)} %copy-done.3, bf16[2,256,1024]{2,1,0:T(8,128)(2,1)S(1)} %copy-done, bf16[2,256,1024]{2,1,0:T(8,128)(2,1)S(1)} %copy-done.1, s32[1,2]{1,0:T(1,128)S(1)} %bitcast.7, s32[1,2048]{1,0:T(1,128)S(1)} %bitcast.4, s32[2,128]{1,0:T(2,128)S(1)} %bitcast.6), custom_call_target="tpu_custom_call" | custom-call | tf_op jit(solution)/shard_map/attention/pallas_call | solution.py:239
  44.9 0.0 copy-start.2
  45.0 0.7 copy-done.2
  45.7 0.0 copy-start.6
  45.7 0.6 copy-done.6
  46.2 50.5 %experts.1 = bf16[128,1024]{1,0:T(8,128)(2,1)} custom-call(bf16[1024,128]{1,0:T(8,128)(2,1)} %copy-done.2, s32[2,128]{1,0:T(2,128)} %copy-done.6, s32[2,128]{1,0:T(2,128)} %bitcast.5, f32[128,2]{1,0:T(8,128)} %copy.13.gates_ref, bf16[128,1024]{1,0:T(8,128)(2,1)} %states_ref.1, f32[1,1024]{1,0:T(1,128)} %bitcast.8, bf16[1024,1024]{1,0:T(8,128)(2,1)} %wo_hbm.1, ...), custom_call_target="tpu_custom_call" | custom-call | tf_op jit(solution)/shard_map/experts/pallas_call | solution.py:395
  96.7 1.7 %copy.15 = bf16[128,1024]{1,0:T(8,128)(2,1)} copy(bf16[128,1024]{1,0:T(8,128)(2,1)} %experts.1) | data formatting | bytes 524288
Async XLA Ops:
  1.4 1.2 %copy-start = (bf16[2,256,1024]{2,1,0:T(8,128)(2,1)S(1)}, bf16[2,256,1024]{2,1,0:T(8,128)(2,1)}, u32[]{:S(2)}) copy-start(bf16[2,256,1024]{2,1,0:T(8,128)(2,1)} %k_hbm.1) | copy-start | bytes 3145732
  2.6 1.2 %copy-start.1 = (bf16[2,256,1024]{2,1,0:T(8,128)(2,1)S(1)}, bf16[2,256,1024]{2,1,0:T(8,128)(2,1)}, u32[]{:S(2)}) copy-start(bf16[2,256,1024]{2,1,0:T(8,128)(2,1)} %v_hbm.1) | copy-start | bytes 3145732
  3.9 0.9 copy-start.3
  4.8 0.7 copy-start.4
  5.5 0.7 copy-start.5
  6.2 0.7 copy-start.7
  44.9 0.7 copy-start.2
  45.7 0.6 copy-start.6

commit v2 on v1

--- a/solution.py
+++ b/solution.py
@@ -1,4 +1,4 @@
-import functools
+import itertools
 import math
 
 import jax
@@ -13,6 +13,7 @@
 BF = jnp.bfloat16
 F32 = jnp.float32
 LOW = -1e30
+VMEM_ALL = 67043328
 
 FULL = ((0, 1), (0, 3), (1, 0), (3, 0))
 FIRST = ((1, 1), (1, 3), (2, 0))
@@ -28,14 +29,21 @@
     return ((y + 8) % 4) * 4 + (z + 8) % 4
 
 
+def far_first(steps):
+    def hops(step):
+        return sum(min(d, 4 - d) for d in step[:3])
+
+    return sorted((s for s in steps if any(s)), key=lambda s: (-hops(s), sum(s) % 3, s))
+
+
 def cols(head, width=128):
     return pl.ds(pl.multiple_of(head * width, width), width)
 
 
 def attention_kernel(
-    q_hbm, k_hbm, v_hbm, len_ref, user_ref, routes_ref,
+    q_hbm, k_hbm, v_hbm, len_hbm, user_hbm, routes_hbm,
     att_ref, partner_ref,
-    q_v, k_v, v_v, qbuf, kcat, vcat, qt, score, prob, osend, obuf, ssend, sbuf, rbuf,
+    len_ref, user_ref, routes_ref, q_v, k_v, v_v, qbuf, kcat, vcat, qt, score, prob, osend, obuf, ssend, sbuf, rbuf,
     load_sem, own_sem, qs, qr, ks, kr, vs, vr, os, orr, ss, sr, rs, rr,
 ):
     me = lax.axis_index("seq")
@@ -50,7 +58,12 @@
 
     loads = [
         pltpu.make_async_copy(src, dst, load_sem.at[i])
-        for i, (src, dst) in enumerate(((q_hbm, q_v), (k_hbm, k_v), (v_hbm, v_v)))
+        for i, (src, dst) in enumerate(
+            (
+                (q_hbm, q_v), (k_hbm, k_v), (v_hbm, v_v),
+                (routes_hbm, routes_ref), (user_hbm, user_ref), (len_hbm, len_ref),
+            )
+        )
     ]
     for copy in loads:
         copy.start()
@@ -75,24 +88,21 @@
     pl.semaphore_wait(barrier, count - 1)
 
     partner = me + 1 - 2 * (me % 2)
+    loads[3].wait()
     route_copy = pltpu.make_async_remote_copy(
         src_ref=routes_ref, dst_ref=rbuf, send_sem=rs, recv_sem=rr,
         device_id={"seq": partner}, device_id_type=MESH,
     )
+    loads[0].wait()
+    for dy, dz in far_first(itertools.product(range(4), range(4))):
+        ty, tz = (y + dy) % 4, (z + dz) % 4
+        pltpu.make_async_remote_copy(
+            src_ref=q_v.at[:, cols(head_of(ty, tz))],
+            dst_ref=qbuf.at[me],
+            send_sem=qs, recv_sem=qr,
+            device_id={"seq": ty * 4 + tz}, device_id_type=MESH,
+        ).start()
     route_copy.start()
-
-    loads[0].wait()
-    for dy in range(4):
-        for dz in range(4):
-            if dy == 0 and dz == 0:
-                continue
-            ty, tz = (y + dy) % 4, (z + dz) % 4
-            pltpu.make_async_remote_copy(
-                src_ref=q_v.at[:, cols(head_of(ty, tz))],
-                dst_ref=qbuf.at[me],
-                send_sem=qs, recv_sem=qr,
-                device_id={"seq": ty * 4 + tz}, device_id_type=MESH,
-            ).start()
 
     def send_rows(src, dst, send_sem, recv_sem):
         for j, (dy, dz) in enumerate(HALVES):
@@ -128,6 +138,8 @@
         base = seq_of(y + dy, z + dz) * hist
         starts.append(base if (dy, dz) in FIRST else base + half)
 
+    loads[4].wait()
+    loads[5].wait()
     own[0].wait()
     moved = pl.ds(0, count - 1)
     pltpu.make_async_copy(qbuf.at[moved], qbuf.at[moved], qr).wait()
@@ -146,8 +158,8 @@
 
     tokens = count * tok
     block = 4 * tok
-    limit0 = len_ref[0, 0]
-    limit1 = len_ref[0, 1]
+    limit0 = len_ref[0:1, 0:1]
+    limit1 = len_ref[0:1, 1:2]
     stat = {}
     for b in range(tokens // block):
         here = pl.ds(b * block, block)
@@ -232,9 +244,8 @@
     width = model // HEADS
     rows = 8 * hist
     count = 16
-    any_spec = pl.BlockSpec(memory_space=pl.ANY)
+    hbm = pl.BlockSpec(memory_space=pltpu.HBM)
     vmem = pl.BlockSpec(memory_space=pltpu.VMEM)
-    smem = pl.BlockSpec(memory_space=pltpu.SMEM)
     dma = pltpu.SemaphoreType.DMA
     return pl.pallas_call(
         attention_kernel,
@@ -242,9 +253,12 @@
             jax.ShapeDtypeStruct((model, tok), BF),
             jax.ShapeDtypeStruct((2, tok), jnp.int32),
         ),
-        in_specs=[any_spec, any_spec, any_spec, smem, vmem, vmem],
+        in_specs=[hbm] * 6,
         out_specs=(vmem, vmem),
         scratch_shapes=[
+            pltpu.VMEM(lengths.shape, jnp.int32),
+            pltpu.VMEM(users.shape, jnp.int32),
+            pltpu.VMEM((2, tok), jnp.int32),
             pltpu.VMEM((tok, model), BF),
             pltpu.VMEM((2, hist, model), BF),
             pltpu.VMEM((2, hist, model), BF),
@@ -259,21 +273,22 @@
             pltpu.VMEM((count, 8, tok), F32),
             pltpu.VMEM((count, 8, tok), F32),
             pltpu.VMEM((2, tok), jnp.int32),
-            dma((3,)),
+            dma((6,)),
             dma((5,)),
         ]
         + [dma] * 12,
         compiler_params=pltpu.CompilerParams(
-            collective_id=0, has_side_effects=True, vmem_limit_bytes=48 * 1024 * 1024
+            collective_id=0, has_side_effects=True, vmem_limit_bytes=VMEM_ALL
         ),
         name="attention",
     )(queries, keys, values, lengths, users, routes)
 
 
 def experts_kernel(
-    att_ref, partner_ref, routes_ref, gates_ref, states_ref, gain_ref, wo_hbm, up_hbm, down_hbm,
+    att_hbm, partner_hbm, routes_hbm, gates_hbm, states_hbm, gain_hbm, wo_hbm, up_hbm, down_hbm,
     out_ref,
-    wo, up, down, send, recv, hidden, back, answer,
+    att_ref, partner_ref, routes_ref, gates_ref, states_ref, gain_ref, wo, up, down,
+    send, recv, partial, hidden, back, answer,
     load_sem, ds, dr, bs, br,
 ):
     s, g = lax.axis_index("seq"), lax.axis_index("grp")
@@ -284,12 +299,21 @@
     pair = g * (seqs // 2) + s // 2
     tok, model = states_ref.shape
     ff = up.shape[1]
+    parts = send.shape[0]
+    part = model // parts
     loads = [
         pltpu.make_async_copy(src, dst, load_sem.at[i])
-        for i, (src, dst) in enumerate(((wo_hbm, wo), (up_hbm.at[0], up), (down_hbm.at[0], down)))
+        for i, (src, dst) in enumerate(
+            (
+                (routes_hbm, routes_ref), (wo_hbm, wo), (states_hbm, states_ref),
+                (gain_hbm, gain_ref), (gates_hbm, gates_ref),
+                (up_hbm.at[0], up), (down_hbm.at[0], down),
+                (att_hbm, att_ref), (partner_hbm, partner_ref),
+            )
+        )
     ]
-    for copy in loads:
-        copy.start()
+    for i in (0, 8, 7, 1, 2, 3, 4, 5, 6):
+        loads[i].start()
 
     barrier = pltpu.get_barrier_semaphore()
 
@@ -303,14 +327,25 @@
 
     lax.fori_loop(1, total, greet, 0)
 
+    ys = [(s // 4 + d) % 4 * 4 for d in range(4)]
+    zs = [(s + d) % 4 for d in range(4)]
+    xs = [(g // 2 + d) % 4 * 2 for d in range(4)]
+    cs = [(g + d) % 2 for d in range(2)]
+    others = [
+        (ys[dy] + zs[dz], xs[dx] + cs[dc])
+        for dy, dz, dx, dc in far_first(itertools.product(range(4), range(4), range(4), range(2)))
+    ]
+
+    loads[0].wait()
+    loads[8].wait()
     experts = lax.broadcasted_iota(jnp.int32, (total, tok), 0)
     named = [(routes_ref[k : k + 1, :] == experts).astype(F32) for k in range(2)]
-    others = sum((partner_ref[k : k + 1, :] == experts).astype(F32) for k in range(2))
+    theirs = sum((partner_ref[k : k + 1, :] == experts).astype(F32) for k in range(2))
     earlier = (
         lax.broadcasted_iota(jnp.int32, (tok, tok), 0) < lax.broadcasted_iota(jnp.int32, (tok, tok), 1)
     ).astype(BF)
     rank = jnp.dot((named[0] + named[1]).astype(BF), earlier, preferred_element_type=F32)
-    ahead = jnp.dot(others.astype(BF), jnp.ones((tok, tok), BF), preferred_element_type=F32)
+    ahead = jnp.dot(theirs.astype(BF), jnp.ones((tok, tok), BF), preferred_element_type=F32)
     rank = rank + ahead * parity.astype(F32)
     places = lax.broadcasted_iota(jnp.int32, (4 * total, tok), 0)
     onehot = []
@@ -320,97 +355,131 @@
         onehot.append((places == target).astype(F32).astype(BF))
     placed = onehot[0] + onehot[1]
 
-    loads[0].wait()
+    loads[7].wait()
+    loads[1].wait()
+    loads[2].wait()
     residual = states_ref[...].astype(F32) + lax.dot_general(
         att_ref[...], wo[...], (((0,), (0,)), ((), ())), preferred_element_type=F32
     )
     spread = jnp.mean(residual * residual, axis=-1, keepdims=True)
+    loads[3].wait()
     normed = (residual / jnp.sqrt(spread + 1e-06) * gain_ref[...]).astype(BF)
-    send[...] = (
-        jnp.dot(placed, normed, preferred_element_type=F32).reshape(total, 4, model).astype(BF)
-    )
-
-    pl.semaphore_wait(barrier, total - 1)
-
-    def dispatch(i, carry):
-        other = (me + i) % total
-        pltpu.make_async_remote_copy(
-            src_ref=send.at[other], dst_ref=recv.at[parity, pair], send_sem=ds, recv_sem=dr,
-            device_id={"seq": other // grps, "grp": other % grps}, device_id_type=MESH,
-        ).start()
-        return carry
-
-    lax.fori_loop(1, total, dispatch, 0)
-    recv[parity, pair] = send[me]
-    loads[1].wait()
-    loads[2].wait()
-    moved = pl.ds(0, total - 1)
-    pltpu.make_async_copy(answer.at[moved], answer.at[moved], dr).wait()
-    rows = (recv[0].astype(F32) + recv[1].astype(F32)).reshape(2 * total, model).astype(BF)
+
+    def whole(buffer):
+        return buffer.at[pl.ds(0, total - 1)]
+
+    for p in range(parts):
+        send[p] = (
+            jnp.dot(placed, normed[:, p * part : (p + 1) * part], preferred_element_type=F32)
+            .reshape(total, 4, part)
+            .astype(BF)
+        )
+        if p == 0:
+            pl.semaphore_wait(barrier, total - 1)
+        for os, og in others:
+            pltpu.make_async_remote_copy(
+                src_ref=send.at[p, os * grps + og], dst_ref=recv.at[p, parity, pair],
+                send_sem=ds.at[p], recv_sem=dr.at[p],
+                device_id={"seq": os, "grp": og}, device_id_type=MESH,
+            ).start()
+        recv[p, parity, pair] = send[p, me]
+
+    loads[4].wait()
+    gates = [
+        jnp.broadcast_to(gates_ref[k : k + 1, :], (tok, tok)).T for k in range(2)
+    ]
+    loads[5].wait()
+    loads[6].wait()
     step = 512
-    for j in range(ff // step):
-        hidden[:, j * step : (j + 1) * step] = jax.nn.gelu(
-            jnp.dot(rows, up[:, j * step : (j + 1) * step], preferred_element_type=F32)
-        ).astype(BF)
+    for p in range(parts):
+        pltpu.make_async_copy(whole(answer.at[p]), whole(answer.at[p]), dr.at[p]).wait()
+        rows = (
+            (recv[p, 0].astype(F32) + recv[p, 1].astype(F32)).reshape(2 * total, part).astype(BF)
+        )
+        for j in range(ff // step):
+            here = slice(j * step, (j + 1) * step)
+            term = jnp.dot(
+                rows, up[p * part : (p + 1) * part, here], preferred_element_type=F32
+            )
+            if p > 0:
+                term = partial[:, here] + term
+            if p < parts - 1:
+                partial[:, here] = term
+            else:
+                hidden[:, here] = jax.nn.gelu(term).astype(BF)
+
     step = 256
-    for j in range(model // step):
-        back[:, :, j * step : (j + 1) * step] = (
-            jnp.dot(hidden[...], down[:, j * step : (j + 1) * step], preferred_element_type=F32)
-            .reshape(total // 2, 4, step)
-            .astype(BF)
-        )
-
-    def reply(i, carry):
-        other = (me + i) % total
-        os, og = other // grps, other % grps
-        pltpu.make_async_remote_copy(
-            src_ref=back.at[og * (seqs // 2) + os // 2], dst_ref=answer.at[me],
-            send_sem=bs, recv_sem=br,
-            device_id={"seq": os, "grp": og}, device_id_type=MESH,
-        ).start()
-        return carry
-
-    lax.fori_loop(1, total, reply, 0)
-    answer[me] = back[pair]
-    pltpu.make_async_copy(answer.at[moved], answer.at[moved], ds).wait()
-    pltpu.make_async_copy(answer.at[moved], answer.at[moved], bs).wait()
-    pltpu.make_async_copy(answer.at[moved], answer.at[moved], br).wait()
-    answers = answer[...].astype(F32).reshape(4 * total, model).astype(BF)
-    mixed = residual
-    for k in range(2):
-        picked = lax.dot_general(
-            onehot[k], answers, (((0,), (0,)), ((), ())), preferred_element_type=F32
-        )
-        mixed = mixed + picked * gates_ref[:, k : k + 1]
-    out_ref[...] = mixed.astype(BF)
+    for p in range(parts):
+        for j in range(part // step):
+            here = slice(j * step, (j + 1) * step)
+            back[p, :, :, here] = (
+                jnp.dot(
+                    hidden[...], down[:, p * part + j * step : p * part + (j + 1) * step],
+                    preferred_element_type=F32,
+                )
+                .reshape(total // 2, 4, step)
+                .astype(BF)
+            )
+        for os, og in others:
+            pltpu.make_async_remote_copy(
+                src_ref=back.at[p, og * (seqs // 2) + os // 2], dst_ref=answer.at[p, me],
+                send_sem=bs.at[p], recv_sem=br.at[p],
+                device_id={"seq": os, "grp": og}, device_id_type=MESH,
+            ).start()
+        answer[p, me] = back[p, pair]
+
+    for p in range(parts):
+        pltpu.make_async_copy(whole(answer.at[p]), whole(answer.at[p]), ds.at[p]).wait()
+    for p in range(parts):
+        here = slice(p * part, (p + 1) * part)
+        pltpu.make_async_copy(whole(answer.at[p]), whole(answer.at[p]), br.at[p]).wait()
+        answers = answer[p].astype(F32).reshape(4 * total, part).astype(BF)
+        mixed = residual[:, here]
+        for k in range(2):
+            picked = lax.dot_general(
+                onehot[k], answers, (((0,), (0,)), ((), ())), preferred_element_type=F32
+            )
+            mixed = mixed + picked * jnp.concatenate([gates[k]] * (part // tok), axis=1)
+        out_ref[:, here] = mixed.astype(BF)
+    for p in range(parts):
+        pltpu.make_async_copy(whole(answer.at[p]), whole(answer.at[p]), bs.at[p]).wait()
 
 
 def experts(att, partner, routes, gates, states, gain, out_weight, up, down):
     tok, model = states.shape
     ff = up.shape[2]
     total = 128
-    any_spec = pl.BlockSpec(memory_space=pl.ANY)
+    parts = 2
+    part = model // parts
+    hbm = pl.BlockSpec(memory_space=pltpu.HBM)
     vmem = pl.BlockSpec(memory_space=pltpu.VMEM)
     dma = pltpu.SemaphoreType.DMA
     return pl.pallas_call(
         experts_kernel,
         out_shape=jax.ShapeDtypeStruct((tok, model), BF),
-        in_specs=[vmem] * 6 + [any_spec] * 3,
+        in_specs=[hbm] * 9,
         out_specs=vmem,
         scratch_shapes=[
+            pltpu.VMEM((model, tok), BF),
+            pltpu.VMEM((2, tok), jnp.int32),
+            pltpu.VMEM((2, tok), jnp.int32),
+            pltpu.VMEM((2, tok), F32),
+            pltpu.VMEM((tok, model), BF),
+            pltpu.VMEM((1, model), F32),
             pltpu.VMEM((model, model), BF),
             pltpu.VMEM((model, ff), BF),
             pltpu.VMEM((ff, model), BF),
-            pltpu.VMEM((total, 4, model), BF),
-            pltpu.VMEM((2, total // 2, 4, model), BF),
+            pltpu.VMEM((parts, total, 4, part), BF),
+            pltpu.VMEM((parts, 2, total // 2, 4, part), BF),
+            pltpu.VMEM((2 * total, ff), F32),
             pltpu.VMEM((2 * total, ff), BF),
-            pltpu.VMEM((total // 2, 4, model), BF),
-            pltpu.VMEM((total, 4, model), BF),
-            dma((3,)),
+            pltpu.VMEM((parts, total // 2, 4, part), BF),
+            pltpu.VMEM((parts, total, 4, part), BF),
+            dma((9,)),
         ]
-        + [dma] * 4,
+        + [dma((parts,))] * 4,
         compiler_params=pltpu.CompilerParams(
-            collective_id=1, has_side_effects=True, vmem_limit_bytes=56 * 1024 * 1024
+            collective_id=1, has_side_effects=True, vmem_limit_bytes=VMEM_ALL
         ),
         name="experts",
     )(att, partner, routes, gates, states, gain, out_weight, up, down)
@@ -426,7 +495,7 @@
         routes_t,
     )
     return experts(
-        att, partner, routes_t, route_weights, states, norm_gain.reshape(1, -1), out_weight,
+        att, partner, routes_t, route_weights.T, states, norm_gain.reshape(1, -1), out_weight,
         expert_up, expert_down,
     )
 

time: 98.7 us -> 85.8 us (0.87)
  local copies, waits for them, and re-layouts: 9.79 us -> 1.67 us
  Pallas kernels: 88.6 us -> 83.9 us
    unnamed x18 -> x1, local copies, waits for them, and re-layouts: 9.79 us -> 1.67 us
    pallas_call x1, Pallas kernels: 50.5 us -> 47.8 us  [experts(): pl.pallas_call(experts_kernel, out_shape=jax.ShapeDtypeStruct((tok, model...]
    pallas_call x1, Pallas kernels: 38.1 us -> 36.1 us  [attention(): pl.pallas_call(attention_kernel, out_shape=(jax.ShapeDtypeStruct((model,...]
where the time goes in v2:
time: 85.8 us; the launch traced here: 85.6 us
  Pallas kernels  83.9 us (98%)
  local copies, waits for them, and re-layouts  1.67 us (2%)
    pallas_call x1, Pallas kernels, experts(): pl.pallas_call(experts_kernel, out_shape=jax.ShapeDtypeStruct((tok, model...  47.8 us
    pallas_call x1, Pallas kernels, attention(): pl.pallas_call(attention_kernel, out_shape=(jax.ShapeDtypeStruct((model,...  36.1 us

profile of v2, /device:TPU:1, one launch (start us, length us, event | category | flops | bytes accessed | tf_op | source)
XLA Modules:
  0.0 85.6 jit_solution(12685045718258248994)
XLA Ops:
  0.0 36.1 %attention.1 = (bf16[1024,128]{1,0:T(8,128)(2,1)}, s32[2,128]{1,0:T(2,128)}) custom-call(bf16[128,1024]{1,0:T(8,128)(2,1)} %q_hbm.1, bf16[2,256,1024]{2,1,0:T(8,128)(2,1)} %k_hbm.1, bf16[2,256,1024]{2,1,0:T(8,128)(2,1)} %v_hbm.1, s32[1,2]{1,0:T(1,128)} %bitcast.10, s32[1,2048]{1,0:T(1,128)} %bitcast.5, s32[2,128]{1,0:T(2,128)} %bitcast.6), custom_call_target="tpu_custom_call" | custom-call | tf_op jit(solution)/shard_map/attention/pallas_call | solution.py:250
  36.1 47.8 %experts.1 = bf16[128,1024]{1,0:T(8,128)(2,1)} custom-call(bf16[1024,128]{1,0:T(8,128)(2,1)} %get-tuple-element.7.att_hbm, s32[2,128]{1,0:T(2,128)} %get-tuple-element.8.partner_hbm, s32[2,128]{1,0:T(2,128)} %bitcast.7, f32[2,128]{1,0:T(2,128)} %bitcast.9, bf16[128,1024]{1,0:T(8,128)(2,1)} %states_hbm.1, f32[1,1024]{1,0:T(1,128)} %bitcast.8, ...), custom_call_target="tpu_custom_call" | custom-call | tf_op jit(solution)/shard_map/experts/pallas_call | solution.py:457
  84.0 1.7 %copy.14 = bf16[128,1024]{1,0:T(8,128)(2,1)} copy(bf16[128,1024]{1,0:T(8,128)(2,1)} %experts.1) | data formatting | bytes 524288

commit v3 on v2

v3 whole, which is shorter than its diff:
```python
import itertools
import math

import jax
import jax.numpy as jnp
from jax import lax
from jax.experimental import pallas as pl
from jax.experimental.pallas import tpu as pltpu
from jax.sharding import PartitionSpec as P

HEADS = 8
MESH = pl.DeviceIdType.MESH
BF = jnp.bfloat16
F32 = jnp.float32
LOW = -1e30
VMEM_ALL = 67043328
SEQS = 16
GRPS = 8

FULL = ((0, 1), (0, 3), (1, 0), (3, 0))
FIRST = ((1, 1), (1, 3), (2, 0))
SECOND = ((3, 3), (3, 1), (0, 2))
HALVES = FIRST + SECOND


def head_of(y, z):
    return (y % 2) * 4 + (z + 2 * (y // 2)) % 4


def seq_of(y, z):
    return ((y + 8) % 4) * 4 + (z + 8) % 4


def far_first(steps):
    def hops(step):
        return sum(min(d, 4 - d) for d in step[:3])

    return sorted((s for s in steps if any(s)), key=lambda s: (-hops(s), sum(s) % 3, s))


def cols(head, width=128):
    return pl.ds(pl.multiple_of(head * width, width), width)


def block_kernel(
    q_hbm, k_hbm, v_hbm, len_hbm, user_hbm, routes_hbm, gates_hbm, states_hbm, gain_hbm,
    wo_hbm, up_hbm, down_hbm,
    out_ref,
    len_ref, user_ref, routes_ref, q_v, k_v, v_v, qbuf, kcat, vcat, qt, vt, score, prob, acc,
    osend, obuf, ssend, sbuf, rbuf,
    gates_ref, states_ref, gain_ref, wo, up, down,
    onehot, gate, att, residual, send, recv, partial, hidden, back, answer,
    load_sem, own_sem, qs, qr, ks, kr, vs, vr, os, orr, ss, sr, rs, rr, ds, dr, bs, br, ready,
):
    me, g = lax.axis_index("seq"), lax.axis_index("grp")
    y, z = me // 4, me % 4
    head = head_of(y, z)
    hist = k_hbm.shape[1]
    half = hist // 2
    tok, model = q_hbm.shape
    ff = up.shape[1]
    width = model // HEADS
    scale = math.log2(math.e) / math.sqrt(width)
    total = SEQS * GRPS
    mine = me * GRPS + g
    parity = me % 2
    pair = g * (SEQS // 2) + me // 2
    parts = send.shape[0]
    part = model // parts

    def load(i, src, dst):
        return pltpu.make_async_copy(src, dst, load_sem.at[i])

    loads = [
        load(0, q_hbm, q_v), load(1, k_hbm, k_v), load(2, v_hbm, v_v),
        load(3, routes_hbm, routes_ref), load(4, user_hbm, user_ref), load(5, len_hbm, len_ref),
        load(6, wo_hbm, wo), load(7, states_hbm, states_ref), load(8, gain_hbm, gain_ref),
        load(9, gates_hbm, gates_ref), load(10, up_hbm.at[0], up), load(11, down_hbm.at[0], down),
    ]
    for copy in loads[:6]:
        copy.start()
    own = [pltpu.make_async_copy(q_hbm.at[:, cols(head)], qbuf.at[me], own_sem.at[0])]
    for i, (src, dst) in enumerate(((k_hbm, kcat), (v_hbm, vcat))):
        for user in range(2):
            own.append(
                pltpu.make_async_copy(
                    src.at[user, :, cols(head)],
                    dst.at[pl.ds(0, hist), pl.ds(user * width, width)],
                    own_sem.at[1 + 2 * i + user],
                )
            )
    for copy in own:
        copy.start()

    barrier = pltpu.get_barrier_semaphore()
    seq_peers = [
        seq_of(y + dy, z + dz) for dy, dz in far_first(itertools.product(range(4), range(4)))
    ]
    for other in seq_peers:
        pl.semaphore_signal(barrier, inc=1, device_id={"seq": other}, device_id_type=MESH)
    for step in range(1, GRPS):
        pl.semaphore_signal(
            barrier, inc=1, device_id={"grp": (g + step) % GRPS}, device_id_type=MESH
        )
    pl.semaphore_wait(barrier, SEQS - 1 + GRPS - 1)

    loads[0].wait()
    for dy, dz in far_first(itertools.product(range(4), range(4))):
        ty, tz = (y + dy) % 4, (z + dz) % 4
        pltpu.make_async_remote_copy(
            src_ref=q_v.at[:, cols(head_of(ty, tz))],
            dst_ref=qbuf.at[me],
            send_sem=qs, recv_sem=qr,
            device_id={"seq": ty * 4 + tz}, device_id_type=MESH,
        ).start()

    def send_halves(src, dst, send_sem, recv_sem):
        for j, (dy, dz) in enumerate(HALVES):
            ty, tz = (y - dy + 4) % 4, (z - dz + 4) % 4
            first = 0 if (dy, dz) in FIRST else half
            for user in range(2):
                pltpu.make_async_remote_copy(
                    src_ref=src.at[user, pl.ds(first, half), cols(head_of(ty, tz))],
                    dst_ref=dst.at[pl.ds(5 * hist + j * half, half), pl.ds(user * width, width)],
                    send_sem=send_sem, recv_sem=recv_sem,
                    device_id={"seq": ty * 4 + tz}, device_id_type=MESH,
                ).start()

    def send_fulls(src, dst, send_sem, recv_sem):
        for j, (dy, dz) in enumerate(FULL):
            ty, tz = (y - dy + 4) % 4, (z - dz + 4) % 4
            for user in range(2):
                pltpu.make_async_remote_copy(
                    src_ref=src.at[user, :, cols(head_of(ty, tz))],
                    dst_ref=dst.at[pl.ds((1 + j) * hist, hist), pl.ds(user * width, width)],
                    send_sem=send_sem, recv_sem=recv_sem,
                    device_id={"seq": ty * 4 + tz}, device_id_type=MESH,
                ).start()

    loads[1].wait()
    send_halves(k_v, kcat, ks, kr)
    send_fulls(k_v, kcat, ks, kr)
    loads[2].wait()
    send_halves(v_v, vcat, vs.at[0], vr.at[0])
    send_fulls(v_v, vcat, vs.at[1], vr.at[1])

    partner = me + 1 - 2 * parity
    loads[3].wait()
    route_copy = pltpu.make_async_remote_copy(
        src_ref=routes_ref, dst_ref=rbuf, send_sem=rs, recv_sem=rr,
        device_id={"seq": partner}, device_id_type=MESH,
    )
    route_copy.start()
    for other in seq_peers:
        pl.semaphore_signal(ready, inc=1, device_id={"seq": other}, device_id_type=MESH)
    for copy in loads[6:]:
        copy.start()

    starts = []
    for dy, dz in ((0, 0),) + FULL:
        base = seq_of(y + dy, z + dz) * hist
        starts += [base, base + half]
    for dy, dz in HALVES:
        base = seq_of(y + dy, z + dz) * hist
        starts.append(base if (dy, dz) in FIRST else base + half)

    loads[4].wait()
    loads[5].wait()
    own[0].wait()
    moved = pl.ds(0, SEQS - 1)
    pltpu.make_async_copy(qbuf.at[moved], qbuf.at[moved], qr).wait()
    for i in range(SEQS):
        flipped = qbuf[i].T
        users = user_ref[:, i * tok : (i + 1) * tok]
        for user in range(2):
            qt[user * width : (user + 1) * width, i * tok : (i + 1) * tok] = jnp.where(
                users == user, flipped, jnp.zeros_like(flipped)
            )

    route_copy.wait()
    experts = lax.broadcasted_iota(jnp.int32, (total, tok), 0)
    named = [(routes_ref[k : k + 1, :] == experts).astype(F32) for k in range(2)]
    theirs = sum((rbuf[k : k + 1, :] == experts).astype(F32) for k in range(2))
    earlier = (
        lax.broadcasted_iota(jnp.int32, (tok, tok), 0) < lax.broadcasted_iota(jnp.int32, (tok, tok), 1)
    ).astype(BF)
    rank = jnp.dot((named[0] + named[1]).astype(BF), earlier, preferred_element_type=F32)
    ahead = jnp.dot(theirs.astype(BF), jnp.ones((tok, tok), BF), preferred_element_type=F32)
    rank = rank + ahead * parity.astype(F32)
    places = lax.broadcasted_iota(jnp.int32, (4 * total, tok), 0)
    loads[9].wait()
    for k in range(2):
        slot = jnp.sum(named[k] * rank, axis=0, keepdims=True).astype(jnp.int32)
        target = routes_ref[k : k + 1, :] * 4 + slot
        onehot[k] = (places == target).astype(F32).astype(BF)
        gate[k] = jnp.broadcast_to(gates_ref[k : k + 1, :], (tok, tok)).T

    own[1].wait()
    own[2].wait()
    far = pl.ds(5 * hist, 6 * half)
    near = pl.ds(hist, 4 * hist)
    rest = pl.ds(hist, kcat.shape[0] - hist)
    pltpu.make_async_copy(kcat.at[rest], kcat.at[rest], kr).wait()

    block = 4 * tok
    rows_y = [(y + dy) % 4 for dy in (2, 1, 3, 0)]
    limit0 = len_ref[0:1, 0:1]
    limit1 = len_ref[0:1, 1:2]

    def tokens_of(row):
        return pl.ds(pl.multiple_of(row * block, block), block)

    stat = []
    for row in rows_y:
        here = tokens_of(row)
        limit = jnp.where(user_ref[:, here] == 0, limit0, limit1)
        top = jnp.full((8, block), LOW, F32)
        for c, start in enumerate(starts):
            s = jnp.dot(kcat[c * half : (c + 1) * half, :], qt[:, here], preferred_element_type=F32)
            pos = start + lax.broadcasted_iota(jnp.int32, (half, block), 0)
            s = jnp.where(pos < limit, s, LOW)
            score[c * half : (c + 1) * half, :] = s
            top = jnp.maximum(top, s.reshape(half // 8, 8, block).max(0))
        peak = top.max(0, keepdims=True)
        denom = jnp.zeros((8, block), F32)
        for c in range(len(starts)):
            p = jnp.exp2((score[c * half : (c + 1) * half, :] - peak) * scale)
            denom = denom + p.reshape(half // 8, 8, block).sum(0)
            prob[c * half : (c + 1) * half, here] = p.astype(BF)
        stat.append((peak, denom.sum(0, keepdims=True)))

    own[3].wait()
    own[4].wait()
    pltpu.make_async_copy(vcat.at[far], vcat.at[far], vr.at[0]).wait()
    split = 5 * hist
    vt[:, split:] = vcat[split:, :].T
    for row in rows_y:
        here = tokens_of(row)
        acc[:, here] = jnp.dot(vt[:, split:], prob[split:, here], preferred_element_type=F32)
    pltpu.make_async_copy(vcat.at[near], vcat.at[near], vr.at[1]).wait()
    vt[:, :split] = vcat[:split, :].T

    for row, (peak, denom) in zip(rows_y, stat):
        here = tokens_of(row)
        both = acc[:, here] + jnp.dot(vt[:, :split], prob[:split, here], preferred_element_type=F32)
        out = jnp.where(user_ref[:, here] == 0, both[:width], both[width:]) * (1.0 / denom)
        out = out.astype(BF)
        packed = jnp.concatenate([peak, denom, jnp.zeros((6, block), F32)], axis=0)
        for i in range(4):
            osend[row * 4 + i] = out[:, i * tok : (i + 1) * tok]
            ssend[row * 4 + i] = packed[:, i * tok : (i + 1) * tok]
        for dz in (2, 1, 3, 0):
            owner = row * 4 + (z + dz) % 4
            if dz == 0 and row is rows_y[-1]:
                continue
            pltpu.make_async_remote_copy(
                src_ref=osend.at[owner], dst_ref=obuf.at[me], send_sem=os, recv_sem=orr,
                device_id={"seq": owner}, device_id_type=MESH,
            ).start()
            pltpu.make_async_remote_copy(
                src_ref=ssend.at[owner], dst_ref=sbuf.at[me], send_sem=ss, recv_sem=sr,
                device_id={"seq": owner}, device_id_type=MESH,
            ).start()

    obuf[me] = osend[me]
    sbuf[me] = ssend[me]
    pltpu.make_async_copy(qbuf.at[moved], qbuf.at[moved], qs).wait()
    pltpu.make_async_copy(kcat.at[rest], kcat.at[rest], ks).wait()
    pltpu.make_async_copy(vcat.at[far], vcat.at[far], vs.at[0]).wait()
    pltpu.make_async_copy(vcat.at[near], vcat.at[near], vs.at[1]).wait()
    for i in (6, 7, 8):
        loads[i].wait()

    ys = [(y + d) % 4 * 4 for d in range(4)]
    zs = [(z + d) % 4 for d in range(4)]
    xs = [(g // 2 + d) % 4 * 2 for d in range(4)]
    cs = [(g + d) % 2 for d in range(2)]
    others = [
        (ys[dy] + zs[dz], xs[dx] + cs[dc])
        for dy, dz, dx, dc in far_first(itertools.product(range(4), range(4), range(4), range(2)))
    ]
    pl.semaphore_wait(ready, SEQS - 1)

    pltpu.make_async_copy(sbuf.at[moved], sbuf.at[moved], sr).wait()
    pltpu.make_async_copy(obuf.at[moved], obuf.at[moved], orr).wait()
    for h in range(HEADS):
        hy, hz = h // 4, h % 4
        first = hy * 4 + hz
        second = (hy + 2) * 4 + (hz + 2) % 4
        m0, d0 = sbuf[first, 0:1], sbuf[first, 1:2]
        m1, d1 = sbuf[second, 0:1], sbuf[second, 1:2]
        top = jnp.maximum(m0, m1)
        w0 = d0 * jnp.exp2((m0 - top) * scale)
        w1 = d1 * jnp.exp2((m1 - top) * scale)
        inverse = 1.0 / (w0 + w1)
        merged = obuf[first].astype(F32) * (w0 * inverse) + obuf[second].astype(F32) * (w1 * inverse)
        att[h * width : (h + 1) * width, :] = merged.astype(BF)

    res = states_ref[...].astype(F32) + lax.dot_general(
        att[...], wo[...], (((0,), (0,)), ((), ())), preferred_element_type=F32
    )
    residual[...] = res
    spread = jnp.mean(res * res, axis=-1, keepdims=True)
    normed = (res / jnp.sqrt(spread + 1e-06) * gain_ref[...]).astype(BF)
    placed = onehot[0] + onehot[1]

    def whole(buffer):
        return buffer.at[pl.ds(0, total - 1)]

    for p in range(parts):
        send[p] = (
            jnp.dot(placed, normed[:, p * part : (p + 1) * part], preferred_element_type=F32)
            .reshape(total, 4, part)
            .astype(BF)
        )
        for other, og in others:
            pltpu.make_async_remote_copy(
                src_ref=send.at[p, other * GRPS + og], dst_ref=recv.at[p, parity, pair],
                send_sem=ds.at[p], recv_sem=dr.at[p],
                device_id={"seq": other, "grp": og}, device_id_type=MESH,
            ).start()
        recv[p, parity, pair] = send[p, mine]

    pltpu.make_async_copy(obuf.at[moved], obuf.at[moved], os).wait()
    pltpu.make_async_copy(sbuf.at[moved], sbuf.at[moved], ss).wait()
    loads[10].wait()
    loads[11].wait()
    step = 512
    for p in range(parts):
        pltpu.make_async_copy(whole(answer.at[p]), whole(answer.at[p]), dr.at[p]).wait()
        rows = (
            (recv[p, 0].astype(F32) + recv[p, 1].astype(F32)).reshape(2 * total, part).astype(BF)
        )
        for j in range(ff // step):
            here = slice(j * step, (j + 1) * step)
            term = jnp.dot(
                rows, up[p * part : (p + 1) * part, here], preferred_element_type=F32
            )
            if p > 0:
                term = partial[:, here] + term
            if p < parts - 1:
                partial[:, here] = term
            else:
                hidden[:, here] = jax.nn.gelu(term).astype(BF)

    step = 256
    for p in range(parts):
        for j in range(part // step):
            here = slice(j * step, (j + 1) * step)
            back[p, :, :, here] = (
                jnp.dot(
                    hidden[...], down[:, p * part + j * step : p * part + (j + 1) * step],
                    preferred_element_type=F32,
                )
                .reshape(total // 2, 4, step)
                .astype(BF)
            )
        for other, og in others:
            pltpu.make_async_remote_copy(
                src_ref=back.at[p, og * (SEQS // 2) + other // 2], dst_ref=answer.at[p, mine],
                send_sem=bs.at[p], recv_sem=br.at[p],
                device_id={"seq": other, "grp": og}, device_id_type=MESH,
            ).start()
        answer[p, mine] = back[p, pair]

    for p in range(parts):
        pltpu.make_async_copy(whole(answer.at[p]), whole(answer.at[p]), ds.at[p]).wait()
    for p in range(parts):
        here = slice(p * part, (p + 1) * part)
        pltpu.make_async_copy(whole(answer.at[p]), whole(answer.at[p]), br.at[p]).wait()
        answers = answer[p].astype(F32).reshape(4 * total, part).astype(BF)
        mixed = residual[:, here]
        for k in range(2):
            picked = lax.dot_general(
                onehot[k], answers, (((0,), (0,)), ((), ())), preferred_element_type=F32
            )
            mixed = mixed + picked * jnp.concatenate([gate[k]] * (part // tok), axis=1)
        out_ref[:, here] = mixed.astype(BF)
    for p in range(parts):
        pltpu.make_async_copy(whole(answer.at[p]), whole(answer.at[p]), bs.at[p]).wait()


def body(
    queries, states, behavior_keys, behavior_values, lengths, user_of, out_weight, norm_gain,
    routes, route_weights, expert_up, expert_down,
):
    tok, model = queries.shape
    hist = behavior_keys.shape[1]
    ff = expert_up.shape[2]
    width = model // HEADS
    held = 8 * hist
    total = SEQS * GRPS
    parts = 2
    part = model // parts
    hbm = pl.BlockSpec(memory_space=pltpu.HBM)
    vmem = pltpu.VMEM
    dma = pltpu.SemaphoreType.DMA
    return pl.pallas_call(
        block_kernel,
        out_shape=jax.ShapeDtypeStruct((tok, model), BF),
        in_specs=[hbm] * 12,
        out_specs=pl.BlockSpec(memory_space=vmem),
        scratch_shapes=[
            vmem((1, 2), jnp.int32),
            vmem((1, SEQS * tok), jnp.int32),
            vmem((2, tok), jnp.int32),
            vmem((tok, model), BF),
            vmem((2, hist, model), BF),
            vmem((2, hist, model), BF),
            vmem((SEQS, tok, width), BF),
            vmem((held, 2 * width), BF),
            vmem((held, 2 * width), BF),
            vmem((2 * width, SEQS * tok), BF),
            vmem((2 * width, held), BF),
            vmem((held, 4 * tok), F32),
            vmem((held, SEQS * tok), BF),
            vmem((2 * width, SEQS * tok), F32),
            vmem((SEQS, width, tok), BF),
            vmem((SEQS, width, tok), BF),
            vmem((SEQS, 8, tok), F32),
            vmem((SEQS, 8, tok), F32),
            vmem((2, tok), jnp.int32),
            vmem((2, tok), F32),
            vmem((tok, model), BF),
            vmem((1, model), F32),
            vmem((model, model), BF),
            vmem((model, ff), BF),
            vmem((ff, model), BF),
            vmem((2, 4 * total, tok), BF),
            vmem((2, tok, tok), F32),
            vmem((model, tok), BF),
            vmem((tok, model), F32),
            vmem((parts, total, 4, part), BF),
            vmem((parts, 2, total // 2, 4, part), BF),
            vmem((2 * total, ff), F32),
            vmem((2 * total, ff), BF),
            vmem((parts, total // 2, 4, part), BF),
            vmem((parts, total, 4, part), BF),
            dma((12,)),
            dma((5,)),
            dma, dma, dma, dma,
            dma((2,)),
            dma((2,)),
            dma, dma, dma, dma, dma, dma,
        ]
        + [dma((parts,))] * 4
        + [pltpu.SemaphoreType.REGULAR],
        compiler_params=pltpu.CompilerParams(
            collective_id=0, has_side_effects=True, vmem_limit_bytes=VMEM_ALL
        ),
        name="decoder_block",
    )(
        queries, behavior_keys, behavior_values, lengths.reshape(1, -1), user_of.reshape(1, -1),
        routes.T, route_weights.T, states, norm_gain.reshape(1, -1), out_weight, expert_up,
        expert_down,
    )


def solution(mesh):
    return jax.shard_map(
        body,
        mesh=mesh,
        in_specs=(
            P(("grp", "seq"), None),
            P(("grp", "seq"), None),
            P("grp", "seq", None),
            P("grp", "seq", None),
            P("grp"),
            P("grp"),
            P(),
            P(),
            P(("grp", "seq"), None),
            P(("grp", "seq"), None),
            P(("seq", "grp"), None, None),
            P(("seq", "grp"), None, None),
        ),
        out_specs=P(("grp", "seq"), None),
        check_vma=False,
    )
```

time: 85.8 us -> 83 us (0.967)
  Pallas kernels: 83.9 us -> 81.1 us
    pallas_call x2 -> x1, Pallas kernels: 83.9 us -> 81.1 us  [body(): pl.pallas_call(block_kernel, out_shape=jax.ShapeDtypeStruct((tok, model),...]
where the time goes in v3:
time: 83 us; the launch traced here: 82.8 us
  Pallas kernels  81.1 us (98%)
  local copies, waits for them, and re-layouts  1.67 us (2%)
    pallas_call x1, Pallas kernels, body(): pl.pallas_call(block_kernel, out_shape=jax.ShapeDtypeStruct((tok, model),...  81.1 us
    unnamed x1, local copies, waits for them, and re-layouts  1.67 us

profile of v3, /device:TPU:1, one launch (start us, length us, event | category | flops | bytes accessed | tf_op | source)
XLA Modules:
  0.0 82.8 jit_solution(8304342785675759446)
XLA Ops:
  0.0 81.1 %decoder_block.1 = bf16[128,1024]{1,0:T(8,128)(2,1)} custom-call(bf16[128,1024]{1,0:T(8,128)(2,1)} %q_hbm.1, bf16[2,256,1024]{2,1,0:T(8,128)(2,1)} %k_hbm.1, bf16[2,256,1024]{2,1,0:T(8,128)(2,1)} %v_hbm.1, s32[1,2]{1,0:T(1,128)} %bitcast.9, s32[1,2048]{1,0:T(1,128)} %bitcast.5, s32[2,128]{1,0:T(2,128)} %bitcast.7, f32[2,128]{1,0:T(2,128)} %bitcast.8, ...), custom_call_target="tpu_custom_call" | custom-call | tf_op jit(solution)/shard_map/decoder_block/pallas_call | solution.py:398
  81.2 1.7 %copy.14 = bf16[128,1024]{1,0:T(8,128)(2,1)} copy(bf16[128,1024]{1,0:T(8,128)(2,1)} %decoder_block.1) | data formatting | bytes 524288

commit v4 on v3

--- a/solution.py
+++ b/solution.py
@@ -22,6 +22,11 @@
 SECOND = ((3, 3), (3, 1), (0, 2))
 HALVES = FIRST + SECOND
 
+GROUPS = (
+    ((2, 2), (1, 1), (3, 3), (2, 0), (0, 2), (1, 3), (3, 1), (0, 0)),
+    ((1, 2), (2, 3), (3, 2), (2, 1), (1, 0), (0, 3), (3, 0), (0, 1)),
+)
+
 
 def head_of(y, z):
     return (y % 2) * 4 + (z + 2 * (y // 2)) % 4
@@ -49,7 +54,7 @@
     len_ref, user_ref, routes_ref, q_v, k_v, v_v, qbuf, kcat, vcat, qt, vt, score, prob, acc,
     osend, obuf, ssend, sbuf, rbuf,
     gates_ref, states_ref, gain_ref, wo, up, down,
-    onehot, gate, att, residual, send, recv, partial, hidden, back, answer,
+    onehot, gate, att, residual, send, recv, hidden, back, answer,
     load_sem, own_sem, qs, qr, ks, kr, vs, vr, os, orr, ss, sr, rs, rr, ds, dr, bs, br, ready,
 ):
     me, g = lax.axis_index("seq"), lax.axis_index("grp")
@@ -64,9 +69,6 @@
     total = SEQS * GRPS
     mine = me * GRPS + g
     parity = me % 2
-    pair = g * (SEQS // 2) + me // 2
-    parts = send.shape[0]
-    part = model // parts
 
     def load(i, src, dst):
         return pltpu.make_async_copy(src, dst, load_sem.at[i])
@@ -104,6 +106,13 @@
         )
     pl.semaphore_wait(barrier, SEQS - 1 + GRPS - 1)
 
+    partner = me + 1 - 2 * parity
+    loads[3].wait()
+    route_copy = pltpu.make_async_remote_copy(
+        src_ref=routes_ref, dst_ref=rbuf, send_sem=rs, recv_sem=rr,
+        device_id={"seq": partner}, device_id_type=MESH,
+    )
+    route_copy.start()
     loads[0].wait()
     for dy, dz in far_first(itertools.product(range(4), range(4))):
         ty, tz = (y + dy) % 4, (z + dz) % 4
@@ -144,13 +153,6 @@
     send_halves(v_v, vcat, vs.at[0], vr.at[0])
     send_fulls(v_v, vcat, vs.at[1], vr.at[1])
 
-    partner = me + 1 - 2 * parity
-    loads[3].wait()
-    route_copy = pltpu.make_async_remote_copy(
-        src_ref=routes_ref, dst_ref=rbuf, send_sem=rs, recv_sem=rr,
-        device_id={"seq": partner}, device_id_type=MESH,
-    )
-    route_copy.start()
     for other in seq_peers:
         pl.semaphore_signal(ready, inc=1, device_id={"seq": other}, device_id_type=MESH)
     for copy in loads[6:]:
@@ -271,14 +273,6 @@
     for i in (6, 7, 8):
         loads[i].wait()
 
-    ys = [(y + d) % 4 * 4 for d in range(4)]
-    zs = [(z + d) % 4 for d in range(4)]
-    xs = [(g // 2 + d) % 4 * 2 for d in range(4)]
-    cs = [(g + d) % 2 for d in range(2)]
-    others = [
-        (ys[dy] + zs[dz], xs[dx] + cs[dc])
-        for dy, dz, dx, dc in far_first(itertools.product(range(4), range(4), range(4), range(2)))
-    ]
     pl.semaphore_wait(ready, SEQS - 1)
 
     pltpu.make_async_copy(sbuf.at[moved], sbuf.at[moved], sr).wait()
@@ -304,80 +298,92 @@
     normed = (res / jnp.sqrt(spread + 1e-06) * gain_ref[...]).astype(BF)
     placed = onehot[0] + onehot[1]
 
-    def whole(buffer):
-        return buffer.at[pl.ds(0, total - 1)]
-
-    for p in range(parts):
-        send[p] = (
-            jnp.dot(placed, normed[:, p * part : (p + 1) * part], preferred_element_type=F32)
-            .reshape(total, 4, part)
-            .astype(BF)
-        )
-        for other, og in others:
-            pltpu.make_async_remote_copy(
-                src_ref=send.at[p, other * GRPS + og], dst_ref=recv.at[p, parity, pair],
-                send_sem=ds.at[p], recv_sem=dr.at[p],
-                device_id={"seq": other, "grp": og}, device_id_type=MESH,
-            ).start()
-        recv[p, parity, pair] = send[p, mine]
+    zh, x, core = z // 2, g // 2, g % 2
+    slots = list(itertools.product(range(8), range(2), range(2)))
+
+    send[...] = (
+        jnp.dot(placed, normed, preferred_element_type=F32).reshape(total, 4, model).astype(BF)
+    )
+    for n, steps in enumerate(GROUPS):
+        for k, hz, hc in slots:
+            dy, dx = steps[k]
+            for low in range(2):
+                other = (y - dy + 4) % 4 * 4 + (zh + hz) % 2 * 2 + low
+                og = (x - dx + 4) % 4 * 2 + (core + hc) % 2
+                slot = k * 4 + hz * 2 + hc
+
+                def start(other=other, og=og, slot=slot, n=n):
+                    pltpu.make_async_remote_copy(
+                        src_ref=send.at[other * GRPS + og], dst_ref=recv.at[n, parity, slot],
+                        send_sem=ds.at[n], recv_sem=dr.at[n],
+                        device_id={"seq": other, "grp": og}, device_id_type=MESH,
+                    ).start()
+
+                if (dy, dx, hz, hc) == (0, 0, 0, 0):
+                    pl.when(parity != low)(start)
+                else:
+                    start()
+        if n == 0:
+            pltpu.make_async_copy(answer.at[pl.ds(0, 63)], answer.at[pl.ds(0, 63)], ds.at[0]).wait()
+    recv[0, parity, 28] = send[mine]
 
     pltpu.make_async_copy(obuf.at[moved], obuf.at[moved], os).wait()
     pltpu.make_async_copy(sbuf.at[moved], sbuf.at[moved], ss).wait()
     loads[10].wait()
     loads[11].wait()
-    step = 512
-    for p in range(parts):
-        pltpu.make_async_copy(whole(answer.at[p]), whole(answer.at[p]), dr.at[p]).wait()
-        rows = (
-            (recv[p, 0].astype(F32) + recv[p, 1].astype(F32)).reshape(2 * total, part).astype(BF)
-        )
+    for n, steps in enumerate(GROUPS):
+        come = pl.ds(0, 63 + n)
+        pltpu.make_async_copy(answer.at[come], answer.at[come], dr.at[n]).wait()
+        rows = (recv[n, 0].astype(F32) + recv[n, 1].astype(F32)).reshape(total, model).astype(BF)
+        step = 512
         for j in range(ff // step):
             here = slice(j * step, (j + 1) * step)
-            term = jnp.dot(
-                rows, up[p * part : (p + 1) * part, here], preferred_element_type=F32
-            )
-            if p > 0:
-                term = partial[:, here] + term
-            if p < parts - 1:
-                partial[:, here] = term
-            else:
-                hidden[:, here] = jax.nn.gelu(term).astype(BF)
-
-    step = 256
-    for p in range(parts):
-        for j in range(part // step):
+            hidden[:, here] = jax.nn.gelu(
+                jnp.dot(rows, up[:, here], preferred_element_type=F32)
+            ).astype(BF)
+        step = 256
+        for j in range(model // step):
             here = slice(j * step, (j + 1) * step)
-            back[p, :, :, here] = (
-                jnp.dot(
-                    hidden[...], down[:, p * part + j * step : p * part + (j + 1) * step],
-                    preferred_element_type=F32,
-                )
-                .reshape(total // 2, 4, step)
+            back[n, :, :, here] = (
+                jnp.dot(hidden[...], down[:, here], preferred_element_type=F32)
+                .reshape(total // 4, 4, step)
                 .astype(BF)
             )
-        for other, og in others:
-            pltpu.make_async_remote_copy(
-                src_ref=back.at[p, og * (SEQS // 2) + other // 2], dst_ref=answer.at[p, mine],
-                send_sem=bs.at[p], recv_sem=br.at[p],
-                device_id={"seq": other, "grp": og}, device_id_type=MESH,
-            ).start()
-        answer[p, mine] = back[p, pair]
-
-    for p in range(parts):
-        pltpu.make_async_copy(whole(answer.at[p]), whole(answer.at[p]), ds.at[p]).wait()
-    for p in range(parts):
-        here = slice(p * part, (p + 1) * part)
-        pltpu.make_async_copy(whole(answer.at[p]), whole(answer.at[p]), br.at[p]).wait()
-        answers = answer[p].astype(F32).reshape(4 * total, part).astype(BF)
+        for k, hz, hc in slots:
+            dy, dx = steps[k]
+            for low in range(2):
+                other = (y + dy) % 4 * 4 + (zh + hz) % 2 * 2 + low
+                og = (x + dx) % 4 * 2 + (core + hc) % 2
+                slot = k * 4 + hz * 2 + hc
+
+                def start(other=other, og=og, slot=slot, n=n):
+                    pltpu.make_async_remote_copy(
+                        src_ref=back.at[n, slot], dst_ref=answer.at[mine],
+                        send_sem=bs, recv_sem=br,
+                        device_id={"seq": other, "grp": og}, device_id_type=MESH,
+                    ).start()
+
+                if (dy, dx, hz, hc) == (0, 0, 0, 0):
+                    pl.when(parity != low)(start)
+                else:
+                    start()
+    answer[mine] = back[0, 28]
+
+    whole = answer.at[pl.ds(0, total - 1)]
+    pltpu.make_async_copy(answer.at[pl.ds(0, 64)], answer.at[pl.ds(0, 64)], ds.at[1]).wait()
+    pltpu.make_async_copy(whole, whole, br).wait()
+    step = 512
+    for j in range(model // step):
+        here = slice(j * step, (j + 1) * step)
+        answers = answer[:, :, here].astype(F32).reshape(4 * total, step).astype(BF)
         mixed = residual[:, here]
         for k in range(2):
             picked = lax.dot_general(
                 onehot[k], answers, (((0,), (0,)), ((), ())), preferred_element_type=F32
             )
-            mixed = mixed + picked * jnp.concatenate([gate[k]] * (part // tok), axis=1)
+            mixed = mixed + picked * jnp.concatenate([gate[k]] * (step // tok), axis=1)
         out_ref[:, here] = mixed.astype(BF)
-    for p in range(parts):
-        pltpu.make_async_copy(whole(answer.at[p]), whole(answer.at[p]), bs.at[p]).wait()
+    pltpu.make_async_copy(whole, whole, bs).wait()
 
 
 def body(
@@ -390,8 +396,6 @@
     width = model // HEADS
     held = 8 * hist
     total = SEQS * GRPS
-    parts = 2
-    part = model // parts
     hbm = pl.BlockSpec(memory_space=pltpu.HBM)
     vmem = pltpu.VMEM
     dma = pltpu.SemaphoreType.DMA
@@ -430,12 +434,11 @@
             vmem((2, tok, tok), F32),
             vmem((model, tok), BF),
             vmem((tok, model), F32),
-            vmem((parts, total, 4, part), BF),
-            vmem((parts, 2, total // 2, 4, part), BF),
-            vmem((2 * total, ff), F32),
-            vmem((2 * total, ff), BF),
-            vmem((parts, total // 2, 4, part), BF),
-            vmem((parts, total, 4, part), BF),
+            vmem((total, 4, model), BF),
+            vmem((2, 2, total // 4, 4, model), BF),
+            vmem((total, ff), BF),
+            vmem((2, total // 4, 4, model), BF),
+            vmem((total, 4, model), BF),
             dma((12,)),
             dma((5,)),
             dma, dma, dma, dma,
@@ -443,7 +446,7 @@
             dma((2,)),
             dma, dma, dma, dma, dma, dma,
         ]
-        + [dma((parts,))] * 4
+        + [dma((2,)), dma((2,)), dma, dma]
         + [pltpu.SemaphoreType.REGULAR],
         compiler_params=pltpu.CompilerParams(
             collective_id=0, has_side_effects=True, vmem_limit_bytes=VMEM_ALL

time: 83 us -> 76.5 us (0.922)
  Pallas kernels: 81.1 us -> 74.6 us
    pallas_call x1, Pallas kernels: 81.1 us -> 74.6 us  [body(): pl.pallas_call(block_kernel, out_shape=jax.ShapeDtypeStruct((tok, model),...]
where the time goes in v4:
time: 76.5 us; the launch traced here: 76.3 us
  Pallas kernels  74.6 us (98%)
  local copies, waits for them, and re-layouts  1.67 us (2%)
    pallas_call x1, Pallas kernels, body(): pl.pallas_call(block_kernel, out_shape=jax.ShapeDtypeStruct((tok, model),...  74.6 us
    unnamed x1, local copies, waits for them, and re-layouts  1.67 us

profile of v4, /device:TPU:1, one launch (start us, length us, event | category | flops | bytes accessed | tf_op | source)
XLA Modules:
  0.0 76.3 jit_solution(4004567111281985453)
XLA Ops:
  0.0 74.6 %decoder_block.1 = bf16[128,1024]{1,0:T(8,128)(2,1)} custom-call(bf16[128,1024]{1,0:T(8,128)(2,1)} %q_hbm.1, bf16[2,256,1024]{2,1,0:T(8,128)(2,1)} %k_hbm.1, bf16[2,256,1024]{2,1,0:T(8,128)(2,1)} %v_hbm.1, s32[1,2]{1,0:T(1,128)} %bitcast.9, s32[1,2048]{1,0:T(1,128)} %bitcast.5, s32[2,128]{1,0:T(2,128)} %bitcast.7, f32[2,128]{1,0:T(2,128)} %bitcast.8, ...), custom_call_target="tpu_custom_call" | custom-call | tf_op jit(solution)/shard_map/decoder_block/pallas_call | solution.py:402
  74.6 1.7 %copy.14 = bf16[128,1024]{1,0:T(8,128)(2,1)} copy(bf16[128,1024]{1,0:T(8,128)(2,1)} %decoder_block.1) | data formatting | bytes 524288

commit v5 on v4

--- a/solution.py
+++ b/solution.py
@@ -23,8 +23,9 @@
 HALVES = FIRST + SECOND
 
 GROUPS = (
-    ((2, 2), (1, 1), (3, 3), (2, 0), (0, 2), (1, 3), (3, 1), (0, 0)),
-    ((1, 2), (2, 3), (3, 2), (2, 1), (1, 0), (0, 3), (3, 0), (0, 1)),
+    ((2, 2), (2, 0), (0, 2), (0, 0)),
+    ((2, 1), (1, 2), (2, 3), (3, 2), (0, 1), (1, 0), (0, 3), (3, 0)),
+    ((1, 1), (3, 3), (1, 3), (3, 1)),
 )
 
 
@@ -247,7 +248,7 @@
         both = acc[:, here] + jnp.dot(vt[:, :split], prob[:split, here], preferred_element_type=F32)
         out = jnp.where(user_ref[:, here] == 0, both[:width], both[width:]) * (1.0 / denom)
         out = out.astype(BF)
-        packed = jnp.concatenate([peak, denom, jnp.zeros((6, block), F32)], axis=0)
+        packed = jnp.concatenate([peak, denom], axis=0)
         for i in range(4):
             osend[row * 4 + i] = out[:, i * tok : (i + 1) * tok]
             ssend[row * 4 + i] = packed[:, i * tok : (i + 1) * tok]
@@ -299,78 +300,81 @@
     placed = onehot[0] + onehot[1]
 
     zh, x, core = z // 2, g // 2, g % 2
-    slots = list(itertools.product(range(8), range(2), range(2)))
+
+    def peers(n, sign):
+        before = sum(len(steps) for steps in GROUPS[:n])
+        for k, (dy, dx) in enumerate(GROUPS[n]):
+            for hz, hc, low in itertools.product(range(2), range(2), range(2)):
+                other = (y + sign * dy + 4) % 4 * 4 + (zh + hz) % 2 * 2 + low
+                og = (x + sign * dx + 4) % 4 * 2 + (core + hc) % 2
+                here = (dy, dx, hz, hc) == (0, 0, 0, 0)
+                yield (before + k) * 4 + hz * 2 + hc, other, og, low if here else None
+
+    home = 4 * [step for steps in GROUPS for step in steps].index((0, 0))
+
+    def remote(n):
+        return answer.at[pl.ds(0, 8 * len(GROUPS[n]) - ((0, 0) in GROUPS[n]))]
 
     send[...] = (
         jnp.dot(placed, normed, preferred_element_type=F32).reshape(total, 4, model).astype(BF)
     )
-    for n, steps in enumerate(GROUPS):
-        for k, hz, hc in slots:
-            dy, dx = steps[k]
-            for low in range(2):
-                other = (y - dy + 4) % 4 * 4 + (zh + hz) % 2 * 2 + low
-                og = (x - dx + 4) % 4 * 2 + (core + hc) % 2
-                slot = k * 4 + hz * 2 + hc
-
-                def start(other=other, og=og, slot=slot, n=n):
-                    pltpu.make_async_remote_copy(
-                        src_ref=send.at[other * GRPS + og], dst_ref=recv.at[n, parity, slot],
-                        send_sem=ds.at[n], recv_sem=dr.at[n],
-                        device_id={"seq": other, "grp": og}, device_id_type=MESH,
-                    ).start()
-
-                if (dy, dx, hz, hc) == (0, 0, 0, 0):
-                    pl.when(parity != low)(start)
-                else:
-                    start()
-        if n == 0:
-            pltpu.make_async_copy(answer.at[pl.ds(0, 63)], answer.at[pl.ds(0, 63)], ds.at[0]).wait()
-    recv[0, parity, 28] = send[mine]
+    for n in range(len(GROUPS)):
+        if n > 0:
+            pltpu.make_async_copy(remote(n - 1), remote(n - 1), ds.at[n - 1]).wait()
+        for slot, other, og, low in peers(n, -1):
+            def start(slot=slot, other=other, og=og, n=n):
+                pltpu.make_async_remote_copy(
+                    src_ref=send.at[other * GRPS + og], dst_ref=recv.at[parity, slot],
+                    send_sem=ds.at[n], recv_sem=dr.at[n],
+                    device_id={"seq": other, "grp": og}, device_id_type=MESH,
+                ).start()
+
+            if low is None:
+                start()
+            else:
+                pl.when(parity != low)(start)
+    recv[parity, home] = send[mine]
 
     pltpu.make_async_copy(obuf.at[moved], obuf.at[moved], os).wait()
     pltpu.make_async_copy(sbuf.at[moved], sbuf.at[moved], ss).wait()
     loads[10].wait()
     loads[11].wait()
     for n, steps in enumerate(GROUPS):
-        come = pl.ds(0, 63 + n)
-        pltpu.make_async_copy(answer.at[come], answer.at[come], dr.at[n]).wait()
-        rows = (recv[n, 0].astype(F32) + recv[n, 1].astype(F32)).reshape(total, model).astype(BF)
+        pltpu.make_async_copy(remote(n), remote(n), dr.at[n]).wait()
+        low = 4 * sum(len(before) for before in GROUPS[:n])
+        held = slice(low, low + 4 * len(steps))
+        count = 16 * len(steps)
+        rows = recv[0, held].astype(F32) + recv[1, held].astype(F32)
+        rows = rows.reshape(count, model).astype(BF)
         step = 512
         for j in range(ff // step):
             here = slice(j * step, (j + 1) * step)
-            hidden[:, here] = jax.nn.gelu(
+            hidden[:count, here] = jax.nn.gelu(
                 jnp.dot(rows, up[:, here], preferred_element_type=F32)
             ).astype(BF)
         step = 256
         for j in range(model // step):
             here = slice(j * step, (j + 1) * step)
-            back[n, :, :, here] = (
-                jnp.dot(hidden[...], down[:, here], preferred_element_type=F32)
-                .reshape(total // 4, 4, step)
+            back[held, :, here] = (
+                jnp.dot(hidden[:count, :], down[:, here], preferred_element_type=F32)
+                .reshape(4 * len(steps), 4, step)
                 .astype(BF)
             )
-        for k, hz, hc in slots:
-            dy, dx = steps[k]
-            for low in range(2):
-                other = (y + dy) % 4 * 4 + (zh + hz) % 2 * 2 + low
-                og = (x + dx) % 4 * 2 + (core + hc) % 2
-                slot = k * 4 + hz * 2 + hc
-
-                def start(other=other, og=og, slot=slot, n=n):
-                    pltpu.make_async_remote_copy(
-                        src_ref=back.at[n, slot], dst_ref=answer.at[mine],
-                        send_sem=bs, recv_sem=br,
-                        device_id={"seq": other, "grp": og}, device_id_type=MESH,
-                    ).start()
-
-                if (dy, dx, hz, hc) == (0, 0, 0, 0):
-                    pl.when(parity != low)(start)
-                else:
-                    start()
-    answer[mine] = back[0, 28]
+        for slot, other, og, low in peers(n, 1):
+            def start(slot=slot, other=other, og=og):
+                pltpu.make_async_remote_copy(
+                    src_ref=back.at[slot], dst_ref=answer.at[mine], send_sem=bs, recv_sem=br,
+                    device_id={"seq": other, "grp": og}, device_id_type=MESH,
+                ).start()
+
+            if low is None:
+                start()
+            else:
+                pl.when(parity != low)(start)
+    answer[mine] = back[home]
 
     whole = answer.at[pl.ds(0, total - 1)]
-    pltpu.make_async_copy(answer.at[pl.ds(0, 64)], answer.at[pl.ds(0, 64)], ds.at[1]).wait()
+    pltpu.make_async_copy(remote(len(GROUPS) - 1), remote(len(GROUPS) - 1), ds.at[len(GROUPS) - 1]).wait()
     pltpu.make_async_copy(whole, whole, br).wait()
     step = 512
     for j in range(model // step):
@@ -421,8 +425,8 @@
             vmem((2 * width, SEQS * tok), F32),
             vmem((SEQS, width, tok), BF),
             vmem((SEQS, width, tok), BF),
-            vmem((SEQS, 8, tok), F32),
-            vmem((SEQS, 8, tok), F32),
+            vmem((SEQS, 2, tok), F32),
+            vmem((SEQS, 2, tok), F32),
             vmem((2, tok), jnp.int32),
             vmem((2, tok), F32),
             vmem((tok, model), BF),
@@ -435,9 +439,9 @@
             vmem((model, tok), BF),
             vmem((tok, model), F32),
             vmem((total, 4, model), BF),
-            vmem((2, 2, total // 4, 4, model), BF),
-            vmem((total, ff), BF),
-            vmem((2, total // 4, 4, model), BF),
+            vmem((2, total // 2, 4, model), BF),
+            vmem((16 * max(len(steps) for steps in GROUPS), ff), BF),
+            vmem((total // 2, 4, model), BF),
             vmem((total, 4, model), BF),
             dma((12,)),
             dma((5,)),
@@ -446,7 +450,7 @@
             dma((2,)),
             dma, dma, dma, dma, dma, dma,
         ]
-        + [dma((2,)), dma((2,)), dma, dma]
+        + [dma((len(GROUPS),)), dma((len(GROUPS),)), dma, dma]
         + [pltpu.SemaphoreType.REGULAR],
         compiler_params=pltpu.CompilerParams(
             collective_id=0, has_side_effects=True, vmem_limit_bytes=VMEM_ALL

time: 76.5 us -> 75.1 us (0.982)
  Pallas kernels: 74.6 us -> 73.2 us
    pallas_call x1, Pallas kernels: 74.6 us -> 73.2 us  [body(): pl.pallas_call(block_kernel, out_shape=jax.ShapeDtypeStruct((tok, model),...]
where the time goes in v5:
time: 75.1 us; the launch traced here: 74.9 us
  Pallas kernels  73.2 us (97%)
  local copies, waits for them, and re-layouts  1.67 us (2%)
    pallas_call x1, Pallas kernels, body(): pl.pallas_call(block_kernel, out_shape=jax.ShapeDtypeStruct((tok, model),...  73.2 us
    unnamed x1, local copies, waits for them, and re-layouts  1.67 us

profile of v5, /device:TPU:1, one launch (start us, length us, event | category | flops | bytes accessed | tf_op | source)
XLA Modules:
  0.0 74.9 jit_solution(11254400026249824747)
XLA Ops:
  0.0 73.2 %decoder_block.1 = bf16[128,1024]{1,0:T(8,128)(2,1)} custom-call(bf16[128,1024]{1,0:T(8,128)(2,1)} %q_hbm.1, bf16[2,256,1024]{2,1,0:T(8,128)(2,1)} %k_hbm.1, bf16[2,256,1024]{2,1,0:T(8,128)(2,1)} %v_hbm.1, s32[1,2]{1,0:T(1,128)} %bitcast.9, s32[1,2048]{1,0:T(1,128)} %bitcast.5, s32[2,128]{1,0:T(2,128)} %bitcast.7, f32[2,128]{1,0:T(2,128)} %bitcast.8, ...), custom_call_target="tpu_custom_call" | custom-call | tf_op jit(solution)/shard_map/decoder_block/pallas_call | solution.py:406
  73.3 1.7 %copy.14 = bf16[128,1024]{1,0:T(8,128)(2,1)} copy(bf16[128,1024]{1,0:T(8,128)(2,1)} %decoder_block.1) | data formatting | bytes 524288
